TPU v7x, 32 devices: a whole 2x2x4 slice. The times are simulated.
32 devices in a mesh: grp: 2 (over y), lat: 4 (over z), lon: 2 (over x), ch: 2 (over core).
Axes of the slice: x: 2, y: 2, z: 4, core: 2. Of those that a mesh axis runs over, the one named last changes fastest.
Arguments:
- noisy_state: bfloat16 [256, 32, 512], P(('grp', 'ch'), 'lat', 'lon'), parts along dimension 0, may hold values from -6 to 6
- kernel_in: bfloat16 [3, 3, 128, 128], replicated, may hold values from -0.1875 to 0.1875
- bias_in: float32 [128], replicated, may hold values from -4 to 4
- kernel_out: bfloat16 [3, 3, 128, 128], replicated, may hold values from -0.1875 to 0.1875
- interp_weight: bfloat16 [64, 128, 128], P(('grp', 'lat', 'lon')), parts along dimension 0, may hold values from -0.5 to 0.5
- observed: bfloat16 [64, 128, 128], P(('grp', 'lat', 'lon'), 'ch'), parts along dimension 0, may hold values from -6 to 6
- obs_precision: bfloat16 [64, 128], P(('grp', 'lat', 'lon')), parts along dimension 0, may hold values from 0.29882812 to 3
- dest_tile: int32 [64], P(('grp', 'lat', 'lon')), parts along dimension 0, may hold values from 0 to 3, as said below
- row_offset: int32 [64], P(('grp', 'lat', 'lon')), parts along dimension 0, may hold values from 0 to 4
- col_offset: int32 [64], P(('grp', 'lat', 'lon')), parts along dimension 0, may hold values from 0 to 224
Outputs:
- next_state: float32 [256, 32, 512], P(('grp', 'ch'), 'lat', 'lon'), parts along dimension 0
- innovation: bfloat16 [64, 128, 128], P(('grp', 'lat', 'lon'), 'ch'), parts along dimension 0
There are 2 independent parts, one for each index of `grp`. A program takes and returns all parts, laid end to end along the dimension named above; an argument that names none is the same for every part. Nothing has to cross between parts.
Inputs may be any that keep to these rules, and one draw needn't show every extreme that they name: `dest_tile`: the 4 blocks of one device name any one latitude tile at most 2 times; a block's tile lies in the longitude column of the device that holds the block.
All inputs are finite; a program needn't handle non-finite values.
Results may differ from a plain program's by a relative error of at most 0.0085.
Values may be sent and summed in bfloat16 or wider, within the bound.
No kernel may reach another device: no remote copies, remote signals or barrier semaphores. Data moves between devices by JAX's collectives and lax.ppermute only.
A program may use at most 64 MiB of HBM per device.

v0:
```python
import jax
import jax.numpy as jnp
from jax import lax
from jax.sharding import PartitionSpec as P

OBS = 128
PH = 4
PW = 32
CAP = 2


keep_rate = 0.6
blend_rate = 0.4
guide_rate = 0.3


def extended(shard, sides, width):
    for axis, dim in sides:
        size, length = (lax.axis_size(axis), shard.shape[dim])
        up = [(i, (i + 1) % size) for i in range(size)]
        down = [(j, i) for i, j in up]
        last = lax.slice_in_dim(shard, length - width, length, axis=dim)
        initial = lax.slice_in_dim(shard, 0, width, axis=dim)
        before = lax.ppermute(last, axis, up)
        after = lax.ppermute(initial, axis, down)
        shard = jnp.concatenate([before, shard, after], axis=dim)
    return shard


def with_rims(grid_field):
    padded = extended(grid_field, (("lat", 1), ("lon", 2)), 1)
    position = lax.axis_index("lat")
    lat_count = lax.axis_size("lat")
    levels = lax.broadcasted_iota(jnp.int32, (1, padded.shape[1], 1), 1)
    inside = ((levels > 0) | (position > 0)) & (
        (levels < padded.shape[1] - 1) | (position < lat_count - 1)
    )
    return jnp.where(inside, padded, jnp.zeros((), padded.dtype))


def apply_taps(running, kernel_part, padded, grid_rows, grid_cols):
    in_count = padded.shape[0]
    out_count = kernel_part.shape[2]
    for tap_row in range(3):
        stacked = jnp.concatenate(
            [
                padded[:, tap_row : tap_row + grid_rows, tap_col : tap_col + grid_cols]
                for tap_col in range(3)
            ],
            axis=0,
        )
        row_kernel = jnp.transpose(kernel_part[tap_row], (1, 0, 2)).reshape(out_count, 3 * in_count)
        running = running + jnp.einsum(
            "oi,ihw->ohw", row_kernel, stacked, preferred_element_type=jnp.float32
        )
    return running


def convolve(grid_field, kernel_rows):
    padded = with_rims(grid_field)
    grid_rows, grid_cols = (grid_field.shape[1], grid_field.shape[2])
    initial = jnp.zeros((kernel_rows.shape[2], grid_rows, grid_cols), jnp.float32)
    return apply_taps(
        initial, kernel_rows, lax.all_gather(padded, "ch", axis=0, tiled=True), grid_rows, grid_cols
    )


def forward_rows(kernel, first_channel, own_channels):
    return lax.dynamic_slice_in_dim(kernel, first_channel, own_channels, 2)


def adjoint_rows(kernel, first_channel, own_channels):
    columns = lax.dynamic_slice_in_dim(kernel, first_channel, own_channels, 3)
    return jnp.transpose(columns[::-1, ::-1], (0, 1, 3, 2))


def extract(grid_field, patch_rows, patch_cols):

    def take_one(row_start, col_start):
        return lax.dynamic_slice(
            grid_field,
            (jnp.zeros((), jnp.int32), row_start, col_start),
            (grid_field.shape[0], PH, PW),
        )

    return jax.vmap(take_one)(patch_rows, patch_cols)


def spread(grad_patch, patch_rows, patch_cols, grid_shape):
    cell_rows = patch_rows[:, None, None] + lax.broadcasted_iota(jnp.int32, (1, PH, 1), 1)
    cell_cols = patch_cols[:, None, None] + lax.broadcasted_iota(jnp.int32, (1, 1, PW), 2)
    return (
        jnp.zeros(grid_shape, jnp.float32)
        .at[:, cell_rows, cell_cols]
        .add(jnp.moveaxis(grad_patch, 1, 0))
    )


def slot_plan(dest_tile, lat_tiles):
    blocks = dest_tile.shape[0]
    matches = (dest_tile[:, None] == lax.broadcasted_iota(jnp.int32, (1, lat_tiles), 1)).astype(
        jnp.int32
    )
    before = jnp.cumsum(matches, axis=0) - matches
    slot_rank = jnp.sum(before * matches, axis=1)
    flat_slot = dest_tile * CAP + slot_rank
    filler = (
        jnp.full((lat_tiles * CAP,), blocks, jnp.int32)
        .at[flat_slot]
        .set(lax.iota(jnp.int32, blocks))
    )
    filled = filler < blocks
    source = jnp.minimum(filler, blocks - 1)
    return (flat_slot, source, filled)


def observe(denoised, interp_weight, observed, obs_precision, dest_tile, row_offset, col_offset):
    own_channels = denoised.shape[0]
    grid_shape = denoised.shape
    lat_tiles = lax.axis_size("lat")
    slots = lat_tiles * CAP
    flat_slot, source, filled = slot_plan(dest_tile, lat_tiles)
    rows_out = row_offset[source].reshape(lat_tiles, CAP)
    cols_out = col_offset[source].reshape(lat_tiles, CAP)
    weights_out = jnp.where(
        filled[:, None, None], interp_weight[source], jnp.zeros((), jnp.bfloat16)
    ).reshape(lat_tiles, CAP, OBS, PH * PW)
    values_out = observed[source].reshape(lat_tiles, CAP, own_channels, OBS)
    scale_out = jnp.where(
        filled[:, None], obs_precision[source], jnp.zeros((), jnp.bfloat16)
    ).reshape(lat_tiles, CAP, OBS)
    arrived = (
        lax.all_to_all(weights_out, "lat", split_axis=0, concat_axis=0, tiled=True),
        lax.all_to_all(values_out, "lat", split_axis=0, concat_axis=0, tiled=True),
        lax.all_to_all(scale_out, "lat", split_axis=0, concat_axis=0, tiled=True),
        lax.all_to_all(rows_out, "lat", split_axis=0, concat_axis=0, tiled=True),
        lax.all_to_all(cols_out, "lat", split_axis=0, concat_axis=0, tiled=True),
    )
    weights_in = arrived[0].reshape(slots, OBS, PH * PW)
    values_in = arrived[1].reshape(slots, own_channels, OBS)
    scale_in = arrived[2].reshape(slots, OBS)
    rows_in = arrived[3].reshape(slots)
    cols_in = arrived[4].reshape(slots)
    patches = extract(denoised, rows_in, cols_in).reshape(slots, own_channels, PH * PW)
    predicted = jnp.einsum("scp,sop->sco", patches, weights_in, preferred_element_type=jnp.float32)
    residual = predicted - values_in.astype(jnp.float32)
    rounded = residual.astype(jnp.bfloat16).reshape(lat_tiles, CAP, own_channels, OBS)
    returned = lax.all_to_all(rounded, "lat", split_axis=0, concat_axis=0, tiled=True).reshape(
        slots, own_channels, OBS
    )
    innovation = returned[flat_slot]
    weighted = (residual * scale_in.astype(jnp.float32)[:, None, :]).astype(jnp.bfloat16)
    pulled = jnp.einsum("sco,sop->scp", weighted, weights_in, preferred_element_type=jnp.float32)
    grad_field = spread(pulled.reshape(slots, own_channels, PH, PW), rows_in, cols_in, grid_shape)
    return (grad_field, innovation)


def body(
    noisy_state,
    kernel_in,
    bias_in,
    kernel_out,
    interp_weight,
    observed,
    obs_precision,
    dest_tile,
    row_offset,
    col_offset,
):
    own_channels = noisy_state.shape[0]
    first_channel = lax.axis_index("ch") * own_channels
    bias_local = lax.dynamic_slice_in_dim(bias_in, first_channel, own_channels, 0)
    pre_act = (
        convolve(noisy_state, forward_rows(kernel_in, first_channel, own_channels))
        + bias_local[:, None, None]
    )
    hidden = jax.nn.silu(pre_act).astype(jnp.bfloat16)
    denoised = (
        noisy_state.astype(jnp.float32)
        + convolve(hidden, forward_rows(kernel_out, first_channel, own_channels))
    ).astype(jnp.bfloat16)
    grad_field, innovation = observe(
        denoised, interp_weight, observed, obs_precision, dest_tile, row_offset, col_offset
    )
    grad_round = grad_field.astype(jnp.bfloat16)
    back_hidden = convolve(grad_round, adjoint_rows(kernel_out, first_channel, own_channels))
    sigmoid_act = jax.nn.sigmoid(pre_act)
    grad_pre = (back_hidden * sigmoid_act * (1.0 + pre_act * (1.0 - sigmoid_act))).astype(
        jnp.bfloat16
    )
    grad_state = grad_field + convolve(
        grad_pre, adjoint_rows(kernel_in, first_channel, own_channels)
    )
    next_state = (
        keep_rate * noisy_state.astype(jnp.float32)
        + blend_rate * denoised.astype(jnp.float32)
        - guide_rate * grad_state
    )
    return (next_state, innovation)


def solution(mesh):
    return jax.shard_map(
        body,
        mesh=mesh,
        in_specs=(
            P(("grp", "ch"), "lat", "lon"),
            P(),
            P(),
            P(),
            P(("grp", "lat", "lon"), None, None),
            P(("grp", "lat", "lon"), "ch", None),
            P(("grp", "lat", "lon"), None),
            P(("grp", "lat", "lon")),
            P(("grp", "lat", "lon")),
            P(("grp", "lat", "lon")),
        ),
        out_specs=(P(("grp", "ch"), "lat", "lon"), P(("grp", "lat", "lon"), "ch", None)),
        check_vma=False,
    )
```

profile of v0, /device:TPU:0, one launch (start us, length us, event | category | flops | bytes accessed | tf_op | source)
XLA Modules:
  0.0 143.8 jit_solution(14844164952837276044)
XLA Ops:
  0.7 1.2 fusion.163
  1.9 3.1 %collective-permute-start = (bf16[64,1,256]{2,0,1:T(8,128)(2,1)S(1)}, bf16[64,1,256]{2,0,1:T(8,128)(2,1)S(1)}, u32[]{:S(2)}, u32[]{:S(2)}) collective-permute-start(bf16[64,1,256]{2,0,1:T(8,128)(2,1)S(1)} %copy.179), channel_id=1, source_target_pairs={{0,4},{4,8},{8,12},{12,0},{1,5},{5,9},{9,13},{13,1},{2,6},{6,10},{... | collective-permute-start | bytes 98312 | tf_op jit(solution)/shard_map/ppermute | solution.py:24
  5.0 2.1 %collective-permute-start.1 = (bf16[64,1,256]{2,0,1:T(8,128)(2,1)S(1)}, bf16[64,1,256]{2,0,1:T(8,128)(2,1)S(1)}, u32[]{:S(2)}, u32[]{:S(2)}) collective-permute-start(bf16[64,1,256]{2,0,1:T(8,128)(2,1)S(1)} %copy.180), channel_id=1, source_target_pairs={{4,0},{8,4},{12,8},{0,12},{5,1},{9,5},{13,9},{1,13},{6,2},{10,6},{... | collective-permute-start | bytes 98312 | tf_op jit(solution)/shard_map/ppermute | solution.py:25
  7.1 0.7 fusion.134
  7.9 0.8 select_reduce_fusion
  8.7 0.7 compare_select_fusion.5
  10.0 1.3 gather_fusion.1
  11.3 0.7 all_to_all.26
  12.0 3.2 %all-to-all-start.1 = ((s32[4,1,2]{2,1,0:T(1,128)}), s32[4,1,2]{2,1,0:T(1,128)S(1)}, u32[]{:S(2)}, u32[]{:S(2)}) async-start(s32[4,1,2]{2,1,0:T(1,128)} %bitcast.13), calls=%async_computation.1 | async-start | bytes 4096 | tf_op jit(solution)/shard_map/all_to_all | solution.py:137
  16.3 0.6 gather_fusion
  17.0 0.7 all_to_all.24
  18.3 1.2 gather_fusion.3
  20.1 0.8 broadcast_select_fusion
  20.9 0.7 broadcast_select_fusion.2
  21.6 5.1 %all-to-all-start = ((s32[4,1,2]{2,1,0:T(1,128)}), s32[4,1,2]{2,1,0:T(1,128)S(1)}, u32[]{:S(2)}, u32[]{:S(2)}) async-start(s32[4,1,2]{2,1,0:T(1,128)} %bitcast.12), calls=%async_computation | async-start | bytes 4096 | tf_op jit(solution)/shard_map/all_to_all | solution.py:136
  27.2 0.7 reduce.14
  28.0 4.2 %all-to-all-done = s32[4,1,2]{2,1,0:T(1,128)S(1)} async-done(((s32[4,1,2]{2,1,0:T(1,128)}), s32[4,1,2]{2,1,0:T(1,128)S(1)}, u32[]{:S(2)}, u32[]{:S(2)}) %all-to-all-start) | async-done | bytes 64 | tf_op jit(solution)/shard_map/all_to_all | solution.py:136
  32.2 3.2 %all-to-all-start.4 = ((bf16[4,2,128]{2,1,0:T(2,128)(2,1)}), bf16[4,2,128]{2,1,0:T(2,128)(2,1)S(1)}, u32[]{:S(2)}, u32[]{:S(2)}) async-start(bf16[4,2,128]{2,1,0:T(2,128)(2,1)} %broadcast_select_fusion.2), calls=%async_computation.4 | async-start | bytes 4096 | tf_op jit(solution)/shard_map/all_to_all | solution.py:135
  35.4 0.7 reduce.15
  36.7 1.7 %collective-permute-start.2 = (bf16[64,10,1]{2,0,1:T(8,128)(2,1)S(1)}, bf16[64,10,1]{2,0,1:T(8,128)(2,1)S(1)}, u32[]{:S(2)}, u32[]{:S(2)}) collective-permute-start(bf16[64,10,1]{2,0,1:T(8,128)(2,1)S(1)} %get-tuple-element.98), channel_id=1, source_target_pairs={{0,2},{2,0},{1,3},{3,1},{4,6},{6,4},{5,7},{7,5},{8,10},{10,8},{9,1... | collective-permute-start | bytes 3848 | tf_op jit(solution)/shard_map/ppermute | solution.py:24
  38.9 3.5 %collective-permute-done.2 = bf16[64,10,1]{2,0,1:T(8,128)(2,1)S(1)} collective-permute-done((bf16[64,10,1]{2,0,1:T(8,128)(2,1)S(1)}, bf16[64,10,1]{2,0,1:T(8,128)(2,1)S(1)}, u32[]{:S(2)}, u32[]{:S(2)}) %collective-permute-start.2) | collective-permute-done | bytes 1312 | tf_op jit(solution)/shard_map/ppermute | solution.py:24
  42.4 1.8 %collective-permute-done.3 = bf16[64,10,1]{2,0,1:T(8,128)(2,1)S(1)} collective-permute-done((bf16[64,10,1]{2,0,1:T(8,128)(2,1)S(1)}, bf16[64,10,1]{2,0,1:T(8,128)(2,1)S(1)}, u32[]{:S(2)}, u32[]{:S(2)}) %collective-permute-start.3) | collective-permute-done | bytes 1312 | tf_op jit(solution)/shard_map/ppermute | solution.py:25
  44.5 2.5 %all_gather.12 = bf16[128,10,258]{2,0,1:T(8,128)(2,1)S(1)} all-gather(bf16[64,10,258]{2,0,1:T(8,128)(2,1)S(1)} %maximum_select_fusion), channel_id=1, replica_groups=mesh['grp'=2,'lat'=4,'lon'=2,'ch'=2] {'ch'}, dimensions={0}, use_global_device_ids=true | all-gather | bytes 990720 | tf_op jit(solution)/shard_map/all_gather | solution.py:64
  47.0 1.2 fusion.153
  49.0 1.2 multiply_convert_fusion
  50.2 1.7 %collective-permute-start.4 = (bf16[64,1,256]{2,0,1:T(8,128)(2,1)S(1)}, bf16[64,1,256]{2,0,1:T(8,128)(2,1)S(1)}, u32[]{:S(2)}, u32[]{:S(2)}) collective-permute-start(bf16[64,1,256]{2,0,1:T(8,128)(2,1)S(1)} %get-tuple-element.116), channel_id=1, source_target_pairs={{0,4},{4,8},{8,12},{12,0},{1,5},{5,9},{9,13},{13,1},{2,6},{6,10},{... | collective-permute-start | bytes 98312 | tf_op jit(solution)/shard_map/ppermute | solution.py:24
  51.9 2.1 %collective-permute-start.5 = (bf16[64,1,256]{2,0,1:T(8,128)(2,1)S(1)}, bf16[64,1,256]{2,0,1:T(8,128)(2,1)S(1)}, u32[]{:S(2)}, u32[]{:S(2)}) collective-permute-start(bf16[64,1,256]{2,0,1:T(8,128)(2,1)S(1)} %get-tuple-element.117), channel_id=1, source_target_pairs={{4,0},{8,4},{12,8},{0,12},{5,1},{9,5},{13,9},{1,13},{6,2},{10,6},{... | collective-permute-start | bytes 98312 | tf_op jit(solution)/shard_map/ppermute | solution.py:25
  54.1 2.0 %collective-permute-done.4 = bf16[64,1,256]{2,0,1:T(8,128)(2,1)S(1)} collective-permute-done((bf16[64,1,256]{2,0,1:T(8,128)(2,1)S(1)}, bf16[64,1,256]{2,0,1:T(8,128)(2,1)S(1)}, u32[]{:S(2)}, u32[]{:S(2)}) %collective-permute-start.4) | collective-permute-done | bytes 32800 | tf_op jit(solution)/shard_map/ppermute | solution.py:24
  56.4 1.6 %collective-permute-start.6 = (bf16[64,10,1]{2,0,1:T(8,128)(2,1)S(1)}, bf16[64,10,1]{2,0,1:T(8,128)(2,1)S(1)}, u32[]{:S(2)}, u32[]{:S(2)}) collective-permute-start(bf16[64,10,1]{2,0,1:T(8,128)(2,1)S(1)} %get-tuple-element.96), channel_id=1, source_target_pairs={{0,2},{2,0},{1,3},{3,1},{4,6},{6,4},{5,7},{7,5},{8,10},{10,8},{9,1... | collective-permute-start | bytes 3848 | tf_op jit(solution)/shard_map/ppermute | solution.py:24
  58.6 4.8 %all-to-all-start.3 = ((bf16[4,2,64,128]{3,2,1,0:T(8,128)(2,1)}), bf16[4,2,64,128]{3,2,1,0:T(8,128)(2,1)S(1)}, u32[]{:S(2)}, u32[]{:S(2)}) async-start(bf16[4,2,64,128]{3,2,1,0:T(8,128)(2,1)} %bitcast.17), calls=%async_computation.3 | async-start | bytes 262144 | tf_op jit(solution)/shard_map/all_to_all | solution.py:134
  63.4 1.4 collective-permute-done.7
  65.1 2.5 %all_gather.13 = bf16[128,10,258]{2,0,1:T(8,128)(2,1)S(1)} all-gather(bf16[64,10,258]{2,0,1:T(8,128)(2,1)S(1)} %maximum_select_fusion.1), channel_id=1, replica_groups=mesh['grp'=2,'lat'=4,'lon'=2,'ch'=2] {'ch'}, dimensions={0}, use_global_device_ids=true | all-gather | bytes 990720 | tf_op jit(solution)/shard_map/all_gather | solution.py:64
  67.6 1.2 fusion.152
  70.1 4.8 %all-to-all-start.2 = ((bf16[4,2,128,128]{3,2,1,0:T(8,128)(2,1)}), bf16[4,2,128,128]{3,2,1,0:T(8,128)(2,1)S(1)}, u32[]{:S(2)}, u32[]{:S(2)}) async-start(bf16[4,2,128,128]{3,2,1,0:T(8,128)(2,1)} %broadcast_select_fusion), calls=%async_computation.2 | async-start | bytes 524288 | tf_op jit(solution)/shard_map/all_to_all | solution.py:133
  74.9 18.2 %while.1 = (s32[]{:T(128)}, bf16[64,8,256]{2,0,1:T(8,128)(2,1)S(1)}, s32[8,3]{0,1:T(4,128)S(1)}, bf16[8,64,4,32]{1,3,2,0:T(8,128)(2,1)S(1)}, s32[]{:T(128)}) while((s32[]{:T(128)}, bf16[64,8,256]{2,0,1:T(8,128)(2,1)S(1)}, s32[8,3]{0,1:T(4,128)S(1)}, bf16[8,64,4,32]{1,3,2,0:T(8,128)(2,1)S(1)}, s32[]{:T(128)}) %tuple.87), condition=%wide.while_cond, body=%wide.while_body.sunk | while | flops 2 | bytes 163957 | solution.py:80
  75.6 1.4 constant_dynamic-slice_fusion.7
  77.8 1.4 constant_dynamic-slice_fusion.7
  80.1 1.4 constant_dynamic-slice_fusion.7
  82.4 1.4 constant_dynamic-slice_fusion.7
  84.6 1.4 constant_dynamic-slice_fusion.7
  86.9 1.4 constant_dynamic-slice_fusion.7
  89.2 1.4 constant_dynamic-slice_fusion.7
  91.5 1.4 constant_dynamic-slice_fusion.7
  93.1 1.0 fusion.164
  94.3 6.3 %scatter_custom_fusion.1 = f32[64,2048]{0,1:T(8,128)S(1)} fusion(s32[1024]{0:T(1024)S(1)} %reshape.338, f32[1024,64]{1,0:T(8,128)S(1)} %bitcast.128, f32[]{:T(128)} %constant.30.clone.1), kind=kCustom, calls=%fused_computation.104 | custom fusion | flops 65536 | bytes 524292
  101.0 2.1 %collective-permute-start.8 = (bf16[64,1,256]{2,0,1:T(8,128)(2,1)S(1)}, bf16[64,1,256]{2,0,1:T(8,128)(2,1)S(1)}, u32[]{:S(2)}, u32[]{:S(2)}) collective-permute-start(bf16[64,1,256]{2,0,1:T(8,128)(2,1)S(1)} %get-tuple-element.114), channel_id=1, source_target_pairs={{0,4},{4,8},{8,12},{12,0},{1,5},{5,9},{9,13},{13,1},{2,6},{6,10},{... | collective-permute-start | bytes 98312 | tf_op jit(solution)/shard_map/ppermute | solution.py:24
  103.1 2.0 %collective-permute-start.9 = (bf16[64,1,256]{2,0,1:T(8,128)(2,1)S(1)}, bf16[64,1,256]{2,0,1:T(8,128)(2,1)S(1)}, u32[]{:S(2)}, u32[]{:S(2)}) collective-permute-start(bf16[64,1,256]{2,0,1:T(8,128)(2,1)S(1)} %get-tuple-element.115), channel_id=1, source_target_pairs={{4,0},{8,4},{12,8},{0,12},{5,1},{9,5},{13,9},{1,13},{6,2},{10,6},{... | collective-permute-start | bytes 98312 | tf_op jit(solution)/shard_map/ppermute | solution.py:25
  105.1 1.6 %collective-permute-done.8 = bf16[64,1,256]{2,0,1:T(8,128)(2,1)S(1)} collective-permute-done((bf16[64,1,256]{2,0,1:T(8,128)(2,1)S(1)}, bf16[64,1,256]{2,0,1:T(8,128)(2,1)S(1)}, u32[]{:S(2)}, u32[]{:S(2)}) %collective-permute-start.8) | collective-permute-done | bytes 32800 | tf_op jit(solution)/shard_map/ppermute | solution.py:24
  107.3 1.6 %collective-permute-start.10 = (bf16[64,10,1]{2,0,1:T(8,128)(2,1)S(1)}, bf16[64,10,1]{2,0,1:T(8,128)(2,1)S(1)}, u32[]{:S(2)}, u32[]{:S(2)}) collective-permute-start(bf16[64,10,1]{2,0,1:T(8,128)(2,1)S(1)} %get-tuple-element.94), channel_id=1, source_target_pairs={{0,2},{2,0},{1,3},{3,1},{4,6},{6,4},{5,7},{7,5},{8,10},{10,8},{9,1... | collective-permute-start | bytes 3848 | tf_op jit(solution)/shard_map/ppermute | solution.py:24
  109.4 4.2 %collective-permute-done.10 = bf16[64,10,1]{2,0,1:T(8,128)(2,1)S(1)} collective-permute-done((bf16[64,10,1]{2,0,1:T(8,128)(2,1)S(1)}, bf16[64,10,1]{2,0,1:T(8,128)(2,1)S(1)}, u32[]{:S(2)}, u32[]{:S(2)}) %collective-permute-start.10) | collective-permute-done | bytes 1312 | tf_op jit(solution)/shard_map/ppermute | solution.py:24
  113.6 1.8 %collective-permute-done.11 = bf16[64,10,1]{2,0,1:T(8,128)(2,1)S(1)} collective-permute-done((bf16[64,10,1]{2,0,1:T(8,128)(2,1)S(1)}, bf16[64,10,1]{2,0,1:T(8,128)(2,1)S(1)}, u32[]{:S(2)}, u32[]{:S(2)}) %collective-permute-start.11) | collective-permute-done | bytes 1312 | tf_op jit(solution)/shard_map/ppermute | solution.py:25
  115.7 2.5 %all_gather.14 = bf16[128,10,258]{2,0,1:T(8,128)(2,1)S(1)} all-gather(bf16[64,10,258]{2,0,1:T(8,128)(2,1)S(1)} %maximum_select_fusion.2), channel_id=1, replica_groups=mesh['grp'=2,'lat'=4,'lon'=2,'ch'=2] {'ch'}, dimensions={0}, use_global_device_ids=true | all-gather | bytes 990720 | tf_op jit(solution)/shard_map/all_gather | solution.py:64
  118.2 1.2 fusion.151
  120.2 0.6 copy-done.10
  121.3 1.5 %collective-permute-start.12 = (bf16[64,1,256]{2,0,1:T(8,128)(2,1)S(1)}, bf16[64,1,256]{2,0,1:T(8,128)(2,1)S(1)}, u32[]{:S(2)}, u32[]{:S(2)}) collective-permute-start(bf16[64,1,256]{2,0,1:T(8,128)(2,1)S(1)} %get-tuple-element.112), channel_id=1, source_target_pairs={{0,4},{4,8},{8,12},{12,0},{1,5},{5,9},{9,13},{13,1},{2,6},{6,10},{... | collective-permute-start | bytes 98312 | tf_op jit(solution)/shard_map/ppermute | solution.py:24
  122.8 2.4 %collective-permute-start.13 = (bf16[64,1,256]{2,0,1:T(8,128)(2,1)S(1)}, bf16[64,1,256]{2,0,1:T(8,128)(2,1)S(1)}, u32[]{:S(2)}, u32[]{:S(2)}) collective-permute-start(bf16[64,1,256]{2,0,1:T(8,128)(2,1)S(1)} %get-tuple-element.113), channel_id=1, source_target_pairs={{4,0},{8,4},{12,8},{0,12},{5,1},{9,5},{13,9},{1,13},{6,2},{10,6},{... | collective-permute-start | bytes 98312 | tf_op jit(solution)/shard_map/ppermute | solution.py:25
  125.3 1.9 %collective-permute-done.12 = bf16[64,1,256]{2,0,1:T(8,128)(2,1)S(1)} collective-permute-done((bf16[64,1,256]{2,0,1:T(8,128)(2,1)S(1)}, bf16[64,1,256]{2,0,1:T(8,128)(2,1)S(1)}, u32[]{:S(2)}, u32[]{:S(2)}) %collective-permute-start.12) | collective-permute-done | bytes 32800 | tf_op jit(solution)/shard_map/ppermute | solution.py:24
  127.4 1.6 %collective-permute-start.14 = (bf16[64,10,1]{2,0,1:T(8,128)(2,1)S(1)}, bf16[64,10,1]{2,0,1:T(8,128)(2,1)S(1)}, u32[]{:S(2)}, u32[]{:S(2)}) collective-permute-start(bf16[64,10,1]{2,0,1:T(8,128)(2,1)S(1)} %get-tuple-element.92), channel_id=1, source_target_pairs={{0,2},{2,0},{1,3},{3,1},{4,6},{6,4},{5,7},{7,5},{8,10},{10,8},{9,1... | collective-permute-start | bytes 3848 | tf_op jit(solution)/shard_map/ppermute | solution.py:24
  129.5 5.0 %all-to-all-start.5 = ((bf16[4,2,64,128]{3,2,1,0:T(8,128)(2,1)}), bf16[4,2,64,128]{3,2,1,0:T(8,128)(2,1)S(1)}, u32[]{:S(2)}, u32[]{:S(2)}) async-start(bf16[4,2,64,128]{3,2,1,0:T(8,128)(2,1)} %bitcast.51), calls=%async_computation.5 | async-start | bytes 262144 | tf_op jit(solution)/shard_map/all_to_all | solution.py:148
  134.5 1.7 %collective-permute-done.15 = bf16[64,10,1]{2,0,1:T(8,128)(2,1)S(1)} collective-permute-done((bf16[64,10,1]{2,0,1:T(8,128)(2,1)S(1)}, bf16[64,10,1]{2,0,1:T(8,128)(2,1)S(1)}, u32[]{:S(2)}, u32[]{:S(2)}) %collective-permute-start.15) | collective-permute-done | bytes 1312 | tf_op jit(solution)/shard_map/ppermute | solution.py:25
  136.5 2.5 %all_gather.15 = bf16[128,10,258]{2,0,1:T(8,128)(2,1)S(1)} all-gather(bf16[64,10,258]{2,0,1:T(8,128)(2,1)S(1)} %maximum_select_fusion.3), channel_id=1, replica_groups=mesh['grp'=2,'lat'=4,'lon'=2,'ch'=2] {'ch'}, dimensions={0}, use_global_device_ids=true | all-gather | bytes 990720 | tf_op jit(solution)/shard_map/all_gather | solution.py:64
  139.1 1.2 fusion.150
  141.5 1.1 copy.160
  142.7 1.2 gather_fusion.5
  (160 shorter events, 20.7 us)
Async XLA Ops:
  0.6 17.0 %copy-start = (bf16[4,128,128]{2,1,0:T(8,128)(2,1)S(1)}, bf16[4,128,128]{2,1,0:T(8,128)(2,1)}, u32[]{:S(2)}) copy-start(bf16[4,128,128]{2,1,0:T(8,128)(2,1)} %param.14) | copy-start | bytes 393220
  0.6 14.6 %copy-start.3 = (bf16[3,3,128,128]{3,2,1,0:T(8,128)(2,1)S(1)}, bf16[3,3,128,128]{3,2,1,0:T(8,128)(2,1)}, u32[]{:S(2)}) copy-start(bf16[3,3,128,128]{3,2,1,0:T(8,128)(2,1)} %param.11) | copy-start | bytes 884740
  0.7 14.6 %copy-start.2 = (bf16[3,3,128,128]{3,2,1,0:T(8,128)(2,1)S(1)}, bf16[3,3,128,128]{3,2,1,0:T(8,128)(2,1)}, u32[]{:S(2)}) copy-start(bf16[3,3,128,128]{3,2,1,0:T(8,128)(2,1)} %param.13) | copy-start | bytes 884740
  1.9 34.5 %collective-permute-start = (bf16[64,1,256]{2,0,1:T(8,128)(2,1)S(1)}, bf16[64,1,256]{2,0,1:T(8,128)(2,1)S(1)}, u32[]{:S(2)}, u32[]{:S(2)}) collective-permute-start(bf16[64,1,256]{2,0,1:T(8,128)(2,1)S(1)} %copy.179), channel_id=1, source_target_pairs={{0,4},{4,8},{8,12},{12,0},{1,5},{5,9},{9,13},{13,1},{2,6},{6,10},{... | collective-permute-start | bytes 98312 | tf_op jit(solution)/shard_map/ppermute | solution.py:24
  5.0 31.5 %collective-permute-start.1 = (bf16[64,1,256]{2,0,1:T(8,128)(2,1)S(1)}, bf16[64,1,256]{2,0,1:T(8,128)(2,1)S(1)}, u32[]{:S(2)}, u32[]{:S(2)}) collective-permute-start(bf16[64,1,256]{2,0,1:T(8,128)(2,1)S(1)} %copy.180), channel_id=1, source_target_pairs={{4,0},{8,4},{12,8},{0,12},{5,1},{9,5},{13,9},{1,13},{6,2},{10,6},{... | collective-permute-start | bytes 98312 | tf_op jit(solution)/shard_map/ppermute | solution.py:25
  12.0 9.7 %all-to-all-start.1 = ((s32[4,1,2]{2,1,0:T(1,128)}), s32[4,1,2]{2,1,0:T(1,128)S(1)}, u32[]{:S(2)}, u32[]{:S(2)}) async-start(s32[4,1,2]{2,1,0:T(1,128)} %bitcast.13), calls=%async_computation.1 | async-start | bytes 4096 | tf_op jit(solution)/shard_map/all_to_all | solution.py:137
  15.3 0.7 copy-start.9
  15.3 1.0 copy-start.1
  15.7 2.6 %copy-start.6 = (bf16[4,64,128]{2,1,0:T(8,128)(2,1)S(1)}, bf16[4,64,128]{2,1,0:T(8,128)(2,1)}, u32[]{:S(2)}) copy-start(bf16[4,64,128]{2,1,0:T(8,128)(2,1)} %param.15) | copy-start | bytes 196612
  15.8 3.7 %copy-start.5 = (bf16[4,128]{1,0:T(4,128)(2,1)S(1)}, bf16[4,128]{1,0:T(4,128)(2,1)}, u32[]{:S(2)}) copy-start(bf16[4,128]{1,0:T(4,128)(2,1)} %param.16) | copy-start | bytes 3076
  17.0 19.3 %copy-start.8 = (s32[2]{0:T(128)S(1)}, s32[2]{0:T(128)}, u32[]{:S(2)}) copy-start(s32[2]{0:T(128)} %constant.64) | copy-start | bytes 28
  17.0 19.4 %copy-start.7 = (s32[2]{0:T(128)S(1)}, s32[2]{0:T(128)}, u32[]{:S(2)}) copy-start(s32[2]{0:T(128)} %constant.61) | copy-start | bytes 28
  17.6 18.8 %copy-start.4 = (bf16[64,8,256]{2,1,0:T(8,128)(2,1)S(1)}, bf16[64,8,256]{2,1,0:T(8,128)(2,1)}, u32[]{:S(2)}) copy-start(bf16[64,8,256]{2,1,0:T(8,128)(2,1)} %param.10) | copy-start | bytes 786436
  21.6 10.6 %all-to-all-start = ((s32[4,1,2]{2,1,0:T(1,128)}), s32[4,1,2]{2,1,0:T(1,128)S(1)}, u32[]{:S(2)}, u32[]{:S(2)}) async-start(s32[4,1,2]{2,1,0:T(1,128)} %bitcast.12), calls=%async_computation | async-start | bytes 4096 | tf_op jit(solution)/shard_map/all_to_all | solution.py:136
  32.2 26.4 %all-to-all-start.4 = ((bf16[4,2,128]{2,1,0:T(2,128)(2,1)}), bf16[4,2,128]{2,1,0:T(2,128)(2,1)S(1)}, u32[]{:S(2)}, u32[]{:S(2)}) async-start(bf16[4,2,128]{2,1,0:T(2,128)(2,1)} %broadcast_select_fusion.2), calls=%async_computation.4 | async-start | bytes 4096 | tf_op jit(solution)/shard_map/all_to_all | solution.py:135
  36.7 5.7 %collective-permute-start.2 = (bf16[64,10,1]{2,0,1:T(8,128)(2,1)S(1)}, bf16[64,10,1]{2,0,1:T(8,128)(2,1)S(1)}, u32[]{:S(2)}, u32[]{:S(2)}) collective-permute-start(bf16[64,10,1]{2,0,1:T(8,128)(2,1)S(1)} %get-tuple-element.98), channel_id=1, source_target_pairs={{0,2},{2,0},{1,3},{3,1},{4,6},{6,4},{5,7},{7,5},{8,10},{10,8},{9,1... | collective-permute-start | bytes 3848 | tf_op jit(solution)/shard_map/ppermute | solution.py:24
  38.3 5.8 %collective-permute-start.3 = (bf16[64,10,1]{2,0,1:T(8,128)(2,1)S(1)}, bf16[64,10,1]{2,0,1:T(8,128)(2,1)S(1)}, u32[]{:S(2)}, u32[]{:S(2)}) collective-permute-start(bf16[64,10,1]{2,0,1:T(8,128)(2,1)S(1)} %get-tuple-element.99), channel_id=1, source_target_pairs={{2,0},{0,2},{3,1},{1,3},{6,4},{4,6},{7,5},{5,7},{10,8},{8,10},{11,... | collective-permute-start | bytes 3848 | tf_op jit(solution)/shard_map/ppermute | solution.py:25
  50.2 5.8 %collective-permute-start.4 = (bf16[64,1,256]{2,0,1:T(8,128)(2,1)S(1)}, bf16[64,1,256]{2,0,1:T(8,128)(2,1)S(1)}, u32[]{:S(2)}, u32[]{:S(2)}) collective-permute-start(bf16[64,1,256]{2,0,1:T(8,128)(2,1)S(1)} %get-tuple-element.116), channel_id=1, source_target_pairs={{0,4},{4,8},{8,12},{12,0},{1,5},{5,9},{9,13},{13,1},{2,6},{6,10},{... | collective-permute-start | bytes 98312 | tf_op jit(solution)/shard_map/ppermute | solution.py:24
  51.9 4.3 %collective-permute-start.5 = (bf16[64,1,256]{2,0,1:T(8,128)(2,1)S(1)}, bf16[64,1,256]{2,0,1:T(8,128)(2,1)S(1)}, u32[]{:S(2)}, u32[]{:S(2)}) collective-permute-start(bf16[64,1,256]{2,0,1:T(8,128)(2,1)S(1)} %get-tuple-element.117), channel_id=1, source_target_pairs={{4,0},{8,4},{12,8},{0,12},{5,1},{9,5},{13,9},{1,13},{6,2},{10,6},{... | collective-permute-start | bytes 98312 | tf_op jit(solution)/shard_map/ppermute | solution.py:25
  56.4 7.1 %collective-permute-start.6 = (bf16[64,10,1]{2,0,1:T(8,128)(2,1)S(1)}, bf16[64,10,1]{2,0,1:T(8,128)(2,1)S(1)}, u32[]{:S(2)}, u32[]{:S(2)}) collective-permute-start(bf16[64,10,1]{2,0,1:T(8,128)(2,1)S(1)} %get-tuple-element.96), channel_id=1, source_target_pairs={{0,2},{2,0},{1,3},{3,1},{4,6},{6,4},{5,7},{7,5},{8,10},{10,8},{9,1... | collective-permute-start | bytes 3848 | tf_op jit(solution)/shard_map/ppermute | solution.py:24
  58.0 6.8 %collective-permute-start.7 = (bf16[64,10,1]{2,0,1:T(8,128)(2,1)S(1)}, bf16[64,10,1]{2,0,1:T(8,128)(2,1)S(1)}, u32[]{:S(2)}, u32[]{:S(2)}) collective-permute-start(bf16[64,10,1]{2,0,1:T(8,128)(2,1)S(1)} %get-tuple-element.97), channel_id=1, source_target_pairs={{2,0},{0,2},{3,1},{1,3},{6,4},{4,6},{7,5},{5,7},{10,8},{8,10},{11,... | collective-permute-start | bytes 3848 | tf_op jit(solution)/shard_map/ppermute | solution.py:25
  58.6 11.5 %all-to-all-start.3 = ((bf16[4,2,64,128]{3,2,1,0:T(8,128)(2,1)}), bf16[4,2,64,128]{3,2,1,0:T(8,128)(2,1)S(1)}, u32[]{:S(2)}, u32[]{:S(2)}) async-start(bf16[4,2,64,128]{3,2,1,0:T(8,128)(2,1)} %bitcast.17), calls=%async_computation.3 | async-start | bytes 262144 | tf_op jit(solution)/shard_map/all_to_all | solution.py:134
  70.1 23.0 %all-to-all-start.2 = ((bf16[4,2,128,128]{3,2,1,0:T(8,128)(2,1)}), bf16[4,2,128,128]{3,2,1,0:T(8,128)(2,1)S(1)}, u32[]{:S(2)}, u32[]{:S(2)}) async-start(bf16[4,2,128,128]{3,2,1,0:T(8,128)(2,1)} %broadcast_select_fusion), calls=%async_computation.2 | async-start | bytes 524288 | tf_op jit(solution)/shard_map/all_to_all | solution.py:133
  101.0 5.8 %collective-permute-start.8 = (bf16[64,1,256]{2,0,1:T(8,128)(2,1)S(1)}, bf16[64,1,256]{2,0,1:T(8,128)(2,1)S(1)}, u32[]{:S(2)}, u32[]{:S(2)}) collective-permute-start(bf16[64,1,256]{2,0,1:T(8,128)(2,1)S(1)} %get-tuple-element.114), channel_id=1, source_target_pairs={{0,4},{4,8},{8,12},{12,0},{1,5},{5,9},{9,13},{13,1},{2,6},{6,10},{... | collective-permute-start | bytes 98312 | tf_op jit(solution)/shard_map/ppermute | solution.py:24
  103.1 4.0 %collective-permute-start.9 = (bf16[64,1,256]{2,0,1:T(8,128)(2,1)S(1)}, bf16[64,1,256]{2,0,1:T(8,128)(2,1)S(1)}, u32[]{:S(2)}, u32[]{:S(2)}) collective-permute-start(bf16[64,1,256]{2,0,1:T(8,128)(2,1)S(1)} %get-tuple-element.115), channel_id=1, source_target_pairs={{4,0},{8,4},{12,8},{0,12},{5,1},{9,5},{13,9},{1,13},{6,2},{10,6},{... | collective-permute-start | bytes 98312 | tf_op jit(solution)/shard_map/ppermute | solution.py:25
  107.3 6.3 %collective-permute-start.10 = (bf16[64,10,1]{2,0,1:T(8,128)(2,1)S(1)}, bf16[64,10,1]{2,0,1:T(8,128)(2,1)S(1)}, u32[]{:S(2)}, u32[]{:S(2)}) collective-permute-start(bf16[64,10,1]{2,0,1:T(8,128)(2,1)S(1)} %get-tuple-element.94), channel_id=1, source_target_pairs={{0,2},{2,0},{1,3},{3,1},{4,6},{6,4},{5,7},{7,5},{8,10},{10,8},{9,1... | collective-permute-start | bytes 3848 | tf_op jit(solution)/shard_map/ppermute | solution.py:24
  108.9 6.4 %collective-permute-start.11 = (bf16[64,10,1]{2,0,1:T(8,128)(2,1)S(1)}, bf16[64,10,1]{2,0,1:T(8,128)(2,1)S(1)}, u32[]{:S(2)}, u32[]{:S(2)}) collective-permute-start(bf16[64,10,1]{2,0,1:T(8,128)(2,1)S(1)} %get-tuple-element.95), channel_id=1, source_target_pairs={{2,0},{0,2},{3,1},{1,3},{6,4},{4,6},{7,5},{5,7},{10,8},{8,10},{11,... | collective-permute-start | bytes 3848 | tf_op jit(solution)/shard_map/ppermute | solution.py:25
  119.8 1.0 copy-start.10
  121.3 5.8 %collective-permute-start.12 = (bf16[64,1,256]{2,0,1:T(8,128)(2,1)S(1)}, bf16[64,1,256]{2,0,1:T(8,128)(2,1)S(1)}, u32[]{:S(2)}, u32[]{:S(2)}) collective-permute-start(bf16[64,1,256]{2,0,1:T(8,128)(2,1)S(1)} %get-tuple-element.112), channel_id=1, source_target_pairs={{0,4},{4,8},{8,12},{12,0},{1,5},{5,9},{9,13},{13,1},{2,6},{6,10},{... | collective-permute-start | bytes 98312 | tf_op jit(solution)/shard_map/ppermute | solution.py:24
  122.8 4.4 %collective-permute-start.13 = (bf16[64,1,256]{2,0,1:T(8,128)(2,1)S(1)}, bf16[64,1,256]{2,0,1:T(8,128)(2,1)S(1)}, u32[]{:S(2)}, u32[]{:S(2)}) collective-permute-start(bf16[64,1,256]{2,0,1:T(8,128)(2,1)S(1)} %get-tuple-element.113), channel_id=1, source_target_pairs={{4,0},{8,4},{12,8},{0,12},{5,1},{9,5},{13,9},{1,13},{6,2},{10,6},{... | collective-permute-start | bytes 98312 | tf_op jit(solution)/shard_map/ppermute | solution.py:25
  127.4 7.1 %collective-permute-start.14 = (bf16[64,10,1]{2,0,1:T(8,128)(2,1)S(1)}, bf16[64,10,1]{2,0,1:T(8,128)(2,1)S(1)}, u32[]{:S(2)}, u32[]{:S(2)}) collective-permute-start(bf16[64,10,1]{2,0,1:T(8,128)(2,1)S(1)} %get-tuple-element.92), channel_id=1, source_target_pairs={{0,2},{2,0},{1,3},{3,1},{4,6},{6,4},{5,7},{7,5},{8,10},{10,8},{9,1... | collective-permute-start | bytes 3848 | tf_op jit(solution)/shard_map/ppermute | solution.py:24
  129.0 7.2 %collective-permute-start.15 = (bf16[64,10,1]{2,0,1:T(8,128)(2,1)S(1)}, bf16[64,10,1]{2,0,1:T(8,128)(2,1)S(1)}, u32[]{:S(2)}, u32[]{:S(2)}) collective-permute-start(bf16[64,10,1]{2,0,1:T(8,128)(2,1)S(1)} %get-tuple-element.93), channel_id=1, source_target_pairs={{2,0},{0,2},{3,1},{1,3},{6,4},{4,6},{7,5},{5,7},{10,8},{8,10},{11,... | collective-permute-start | bytes 3848 | tf_op jit(solution)/shard_map/ppermute | solution.py:25
  129.5 13.2 %all-to-all-start.5 = ((bf16[4,2,64,128]{3,2,1,0:T(8,128)(2,1)}), bf16[4,2,64,128]{3,2,1,0:T(8,128)(2,1)S(1)}, u32[]{:S(2)}, u32[]{:S(2)}) async-start(bf16[4,2,64,128]{3,2,1,0:T(8,128)(2,1)} %bitcast.51), calls=%async_computation.5 | async-start | bytes 262144 | tf_op jit(solution)/shard_map/all_to_all | solution.py:148
where the time goes:
time: 145 us; the launch traced here: 144 us
  starting transfers between devices  51.6 us (36%)
  local copies, waits for them, and re-layouts  35.9 us (25%)
  waiting for transfers between devices  24.5 us (17%)
  other arithmetic  13.2 us (9%)
  blocking collectives  10 us (7%)
  matrix products  7.13 us (5%)
    gather x48, local copies, waits for them, and re-layouts  17.9 us
    ppermute x8, starting transfers between devices, extended(): before = lax.ppermute(last, axis, up)  14.8 us
    ppermute x8, waiting for transfers between devices, extended(): before = lax.ppermute(last, axis, up)  13.1 us
    ppermute x8, starting transfers between devices, extended(): after = lax.ppermute(initial, axis, down)  10.6 us
    all_gather x4, blocking collectives, convolve(): lax.all_gather(padded, 'ch', axis=0, tiled=True)  10 us
    ppermute x8, waiting for transfers between devices, extended(): after = lax.ppermute(initial, axis, down)  7.17 us
    unnamed x5, other arithmetic  6.44 us
    dot_general x12, matrix products, apply_taps(): jnp.einsum('oi,ihw->ohw', row_kernel, stacked, preferred_element_type=jnp...  5.9 us
  transfers between devices with their start and end apart: 22, of which 13 were waited for; matrix products, arithmetic and copies ran while one was open for 28% of the time, Pallas kernels for 0%

commit v1 on v0

v1 whole, which is shorter than its diff:
```python
import functools

import jax
import jax.numpy as jnp
from jax import lax
from jax.experimental import pallas as pl
from jax.experimental.pallas import tpu as pltpu
from jax.sharding import PartitionSpec as P

PH = 4
PW = 32
CAP = 2
TAIL = 16
META = 16

keep_rate = 0.6
blend_rate = 0.4
guide_rate = 0.3

F32 = jnp.float32
BF16 = jnp.bfloat16
VMEM = pltpu.VMEM
SMEM = pltpu.SMEM


def call(kernel, out_shape, n_smem, n_vmem, scratch, name):
    return pl.pallas_call(
        kernel,
        out_shape=out_shape,
        in_specs=[pl.BlockSpec(memory_space=SMEM)] * n_smem + [pl.BlockSpec(memory_space=VMEM)] * n_vmem,
        out_specs=jax.tree.map(lambda _: pl.BlockSpec(memory_space=VMEM), out_shape),
        scratch_shapes=scratch,
        name=name,
    )


def weights_kernel(kin_ref, kout_ref, w1_ref, w2_ref, w3_ref, w4_ref):
    c = kin_ref.shape[-1]
    for w_ref, k_ref, adjoint in (
        (w1_ref, kin_ref, False),
        (w2_ref, kout_ref, False),
        (w3_ref, kout_ref, True),
        (w4_ref, kin_ref, True),
    ):
        for b in range(3):
            for row in range(2):
                at = (2 * b + row) * c
                for k in range(4):
                    a = k - row
                    if not 0 <= a < 3:
                        tap = jnp.zeros((c, c), BF16)
                    elif adjoint:
                        tap = k_ref[2 - a, 2 - b]
                    else:
                        tap = k_ref[a, b].astype(F32).T.astype(BF16)
                    w_ref[k * c : (k + 1) * c, at : at + c] = tap


def tail_of(row_ref, width):
    lane_rows = lax.broadcasted_iota(jnp.int32, (TAIL, row_ref.shape[-1]), 0)
    first = row_ref[0:TAIL, :].astype(F32)
    last = row_ref[width - TAIL : width, :].astype(F32)
    zero = jnp.zeros_like(first)
    return jnp.where(lane_rows < 2, first, jnp.where(lane_rows >= TAIL - 2, last, zero)).astype(BF16)


def write_edges(x_ref, top_ref, bottom_ref, tail_ref, tail_top_ref, tail_bottom_ref):
    rows, width = x_ref.shape[0], x_ref.shape[1]
    for i in range(2):
        top_ref[i] = x_ref[i]
        bottom_ref[i] = x_ref[rows - 2 + i]
    for h in range(rows):
        tail_ref[h] = tail_of(x_ref.at[h], width)
    for i in range(2):
        tail_top_ref[i] = tail_ref[i]
        tail_bottom_ref[i] = tail_ref[rows - 2 + i]


def prep_kernel(
    dest_ref,
    row_ref,
    col_ref,
    own_ref,
    other_ref,
    own_obs_ref,
    other_obs_ref,
    weight_ref,
    precision_ref,
    x_ref,
    top_ref,
    bottom_ref,
    tail_ref,
    tail_top_ref,
    tail_bottom_ref,
    chunk_ref,
    flat_ref,
    scale_ref,
):
    core = lax.axis_index("ch")
    half, rows, width = own_ref.shape
    obs = weight_ref.shape[1]
    cells = weight_ref.shape[2]
    blocks = weight_ref.shape[0]

    def place(ref, first):
        for part in range(width // 128):
            piece = ref[:, :, part * 128 : (part + 1) * 128].astype(F32)
            flat_ref[part, pl.ds(pl.multiple_of(first * rows, 8), half * rows), :] = piece.reshape(half * rows, 128)

    place(own_ref, core * half)
    place(other_ref, (1 - core) * half)
    for h in range(rows):
        for part in range(width // 128):
            plane = flat_ref[part, pl.ds(h, 2 * half, stride=rows), :]
            x_ref[h, part * 128 : (part + 1) * 128, :] = plane.T.astype(BF16)
    write_edges(x_ref, top_ref, bottom_ref, tail_ref, tail_top_ref, tail_bottom_ref)

    def clear(slot, _):
        chunk_ref[slot] = jnp.zeros(chunk_ref.shape[1:], BF16)
        return 0

    lax.fori_loop(0, chunk_ref.shape[0], clear, 0)
    scale_ref[...] = precision_ref[...].astype(F32)
    meta_rows = lax.broadcasted_iota(jnp.int32, (META, obs), 0)

    def pack(b, _):
        dest = dest_ref[b]
        rank = lax.fori_loop(0, b, lambda j, n: n + (dest_ref[j] == dest).astype(jnp.int32), 0)
        slot = dest * CAP + rank
        chunk_ref[slot, 0:obs, :] = weight_ref[b]
        chunk_ref[slot, pl.ds(pl.multiple_of(obs + core * half, 16), half), :] = own_obs_ref[b]
        chunk_ref[slot, pl.ds(pl.multiple_of(obs + (1 - core) * half, 16), half), :] = other_obs_ref[b]
        row = row_ref[b].astype(F32)
        high = lax.div(col_ref[b], 16).astype(F32)
        low = lax.rem(col_ref[b], 16).astype(F32)
        meta = jnp.where(
            meta_rows == 0,
            jnp.broadcast_to(scale_ref[pl.ds(b, 1), :], (META, obs)),
            jnp.where(meta_rows == 1, row, jnp.where(meta_rows == 2, high, low)),
        )
        chunk_ref[slot, obs + 2 * half : obs + 2 * half + META, :] = meta.astype(BF16)
        return 0

    lax.fori_loop(0, blocks, pack, 0)


def fill_extended(ext_ref, x_ref, tail_ref, up_ref, up_tail_ref, down_ref, down_tail_ref):
    rows, width = x_ref.shape[0], x_ref.shape[1]
    for i in range(2):
        ext_ref[i, 0:width, :] = up_ref[i]
        ext_ref[i, width : width + TAIL, :] = up_tail_ref[i]
        ext_ref[rows + 2 + i, 0:width, :] = down_ref[i]
        ext_ref[rows + 2 + i, width : width + TAIL, :] = down_tail_ref[i]
    for h in range(rows):
        ext_ref[h + 2, 0:width, :] = x_ref[h]
        ext_ref[h + 2, width : width + TAIL, :] = tail_ref[h]


def row_pair(src_ref, w_ref, first):
    c = src_ref.shape[-1]
    wide = src_ref.shape[1]
    lhs = jnp.concatenate([src_ref[first + k] for k in range(4)], axis=1)
    y = jnp.dot(lhs, w_ref[...], preferred_element_type=F32)
    out = []
    for row in range(2):
        left, mid, right = (y[:, (2 * b + row) * c : (2 * b + row + 1) * c] for b in range(3))
        out.append(pltpu.roll(left, 1, 0) + mid + pltpu.roll(right, wide - 1, 0))
    return out


def inside(ext_row, ext_rows):
    at = lax.axis_index("lat")
    last = lax.axis_size("lat") - 1
    return ((ext_row > 0) | (at > 0)) & ((ext_row < ext_rows - 1) | (at < last))


def forward_kernel(
    x_ref,
    tail_ref,
    up_ref,
    up_tail_ref,
    down_ref,
    down_tail_ref,
    w1_ref,
    w2_ref,
    bias_ref,
    block_ref,
    pre_ref,
    base_ref,
    g_ref,
    top_ref,
    bottom_ref,
    gtail_ref,
    tail_top_ref,
    tail_bottom_ref,
    inn_ref,
    ext_ref,
    hidden_ref,
    den_ref,
    field_ref,
):
    core = lax.axis_index("ch")
    rows, width, c = x_ref.shape
    half = inn_ref.shape[1]
    slots, obs = block_ref.shape[0], block_ref.shape[2]
    fill_extended(ext_ref, x_ref, tail_ref, up_ref, up_tail_ref, down_ref, down_tail_ref)
    bias = bias_ref[...]

    def first_conv(g, _):
        for i, y in enumerate(row_pair(ext_ref, w1_ref, 2 * g)):
            r = 2 * g + i
            pre = y + bias
            pre_ref[r] = pre
            hidden = pre / (1.0 + jnp.exp(-pre))
            hidden_ref[r] = jnp.where(inside(r, rows + 2), hidden, 0.0).astype(BF16)
        return 0

    lax.fori_loop(0, (rows + 2) // 2, first_conv, 0)

    def second_conv(g, _):
        for i, y in enumerate(row_pair(hidden_ref, w2_ref, 2 * g)):
            r = 2 * g + i
            noisy = x_ref[r].astype(F32)
            den = (noisy + y[0:width, :]).astype(BF16).astype(F32)
            den_ref[r] = den
            base_ref[r] = keep_rate * noisy + blend_rate * den
            field_ref[r] = jnp.zeros((width, c), F32)
        return 0

    lax.fori_loop(0, rows // 2, second_conv, 0)

    def observe(slot, _):
        meta = block_ref[slot, obs + c : obs + c + META, :].astype(F32)
        row = jnp.max(meta[1:2, :]).astype(jnp.int32)
        col = jnp.max(meta[2:3, :]).astype(jnp.int32) * 16 + jnp.max(meta[3:4, :]).astype(jnp.int32)
        weight = block_ref[slot, 0:obs, :]
        patch = jnp.concatenate([den_ref[row + i, pl.ds(col, PW), :] for i in range(PH)], axis=0)
        predicted = lax.dot_general(
            patch.T.astype(BF16), weight, (((1,), (1,)), ((), ())), preferred_element_type=F32
        )
        residual = predicted - block_ref[slot, obs : obs + c, :].astype(F32)
        inn_ref[slot] = jnp.where(core == 0, residual[0:half], residual[half : 2 * half]).astype(BF16)
        weighted = (residual * meta[0:1, :]).astype(BF16)
        pulled = jnp.dot(weighted, weight, preferred_element_type=F32).T
        for i in range(PH):
            field_ref[row + i, pl.ds(col, PW), :] += pulled[i * PW : (i + 1) * PW, :]
        return 0

    lax.fori_loop(0, slots, observe, 0)

    for r in range(rows):
        field = field_ref[r]
        base_ref[r] -= guide_rate * field
        g_ref[r] = field.astype(BF16)
    write_edges(g_ref, top_ref, bottom_ref, gtail_ref, tail_top_ref, tail_bottom_ref)


def backward_kernel(
    x_ref,
    tail_ref,
    up_ref,
    up_tail_ref,
    down_ref,
    down_tail_ref,
    w3_ref,
    w4_ref,
    pre_ref,
    base_ref,
    next_ref,
    ext_ref,
    grad_ref,
    flat_ref,
):
    core = lax.axis_index("ch")
    rows, width, c = x_ref.shape
    half = next_ref.shape[0]
    fill_extended(ext_ref, x_ref, tail_ref, up_ref, up_tail_ref, down_ref, down_tail_ref)

    def first_conv(g, _):
        for i, y in enumerate(row_pair(ext_ref, w3_ref, 2 * g)):
            r = 2 * g + i
            pre = pre_ref[r]
            s = 1.0 / (1.0 + jnp.exp(-pre))
            grad = y * s * (1.0 + pre * (1.0 - s))
            grad_ref[r] = jnp.where(inside(r, rows + 2), grad, 0.0).astype(BF16)
        return 0

    lax.fori_loop(0, (rows + 2) // 2, first_conv, 0)

    for g in range(rows // 2):
        for i, y in enumerate(row_pair(grad_ref, w4_ref, 2 * g)):
            r = 2 * g + i
            out = base_ref[r] - guide_rate * y[0:width, :]
            for part in range(width // 128):
                plane = out[part * 128 : (part + 1) * 128, :].T
                own = jnp.where(core == 0, plane[0:half], plane[half : 2 * half])
                flat_ref[part, pl.ds(r, half, stride=rows), :] = own
    for part in range(width // 128):
        next_ref[:, :, part * 128 : (part + 1) * 128] = flat_ref[part].reshape(half, rows, 128)


def return_kernel(dest_ref, back_ref, inn_ref):
    def take(b, _):
        dest = dest_ref[b]
        rank = lax.fori_loop(0, b, lambda j, n: n + (dest_ref[j] == dest).astype(jnp.int32), 0)
        inn_ref[b] = back_ref[dest * CAP + rank]
        return 0

    lax.fori_loop(0, inn_ref.shape[0], take, 0)


def shifted(value, lat_step, lon_step):
    lats, lons = lax.axis_size("lat"), lax.axis_size("lon")
    pairs = [
        (i * lons + j, (i + lat_step) * lons + (j + lon_step) % lons)
        for i in range(lats)
        for j in range(lons)
        if 0 <= i + lat_step < lats
    ]
    return lax.ppermute(value, ("lat", "lon"), pairs)


def tails(value, lat_step):
    if lax.axis_size("lon") == 2:
        return shifted(value, lat_step, 1)
    from_right = shifted(value, lat_step, -1)
    from_left = shifted(value, lat_step, 1)
    at = lax.broadcasted_iota(jnp.int32, (1, TAIL, 1), 1)
    return jnp.where(at < TAIL // 2, from_right, from_left)


def exchanged(top, bottom, tail, tail_top, tail_bottom):
    up = shifted(bottom, 1, 0)
    down = shifted(top, -1, 0)
    beside = tails(tail, 0)
    up_tail = tails(tail_bottom, 1)
    down_tail = tails(tail_top, -1)
    return beside, up, up_tail, down, down_tail


def shape(dims, dtype):
    return jax.ShapeDtypeStruct(dims, dtype)


def edge_shapes(rows, width, c):
    return (
        shape((2, width, c), BF16),
        shape((2, width, c), BF16),
        shape((rows, TAIL, c), BF16),
        shape((2, TAIL, c), BF16),
        shape((2, TAIL, c), BF16),
    )


def body(
    noisy_state,
    kernel_in,
    bias_in,
    kernel_out,
    interp_weight,
    observed,
    obs_precision,
    dest_tile,
    row_offset,
    col_offset,
):
    half, rows, width = noisy_state.shape
    c = kernel_in.shape[-1]
    obs = interp_weight.shape[1]
    lats = lax.axis_size("lat")
    slots = lats * CAP
    wide = width + TAIL
    swap = [(0, 1), (1, 0)]
    other = lax.ppermute(noisy_state, "ch", swap)
    other_obs = lax.ppermute(observed, "ch", swap)
    w1, w2, w3, w4 = call(weights_kernel, (shape((4 * c, 6 * c), BF16),) * 4, 0, 2, [], "weights")(
        kernel_in, kernel_out
    )
    x, *edges, chunk = call(
        prep_kernel,
        (shape((rows, width, c), BF16), *edge_shapes(rows, width, c), shape((slots, obs + c + META, obs), BF16)),
        3,
        6,
        [VMEM((width // 128, c * rows, 128), F32), VMEM(obs_precision.shape, F32)],
        "prep",
    )(dest_tile, row_offset, col_offset, noisy_state, other, observed, other_obs, interp_weight, obs_precision)
    block = lax.all_to_all(chunk, "lat", split_axis=0, concat_axis=0, tiled=True)
    halo = exchanged(*edges)
    pre, base, g, *edges, inn = call(
        forward_kernel,
        (
            shape((rows + 2, wide, c), F32),
            shape((rows, width, c), F32),
            shape((rows, width, c), BF16),
            *edge_shapes(rows, width, c),
            shape((slots, half, obs), BF16),
        ),
        0,
        10,
        [
            VMEM((rows + 4, wide, c), BF16),
            VMEM((rows + 2, wide, c), BF16),
            VMEM((rows, width, c), F32),
            VMEM((rows, width, c), F32),
        ],
        "forward",
    )(x, *halo, w1, w2, bias_in.reshape(1, c), block)
    halo = exchanged(*edges)
    back = lax.all_to_all(inn, "lat", split_axis=0, concat_axis=0, tiled=True)
    next_state = call(
        backward_kernel,
        shape((half, rows, width), F32),
        0,
        10,
        [
            VMEM((rows + 4, wide, c), BF16),
            VMEM((rows + 2, wide, c), BF16),
            VMEM((width // 128, half * rows, 128), F32),
        ],
        "backward",
    )(g, *halo, w3, w4, pre, base)
    innovation = call(return_kernel, shape(observed.shape, BF16), 1, 1, [], "innovation")(dest_tile, back)
    return next_state, innovation


def solution(mesh):
    return jax.shard_map(
        body,
        mesh=mesh,
        in_specs=(
            P(("grp", "ch"), "lat", "lon"),
            P(),
            P(),
            P(),
            P(("grp", "lat", "lon"), None, None),
            P(("grp", "lat", "lon"), "ch", None),
            P(("grp", "lat", "lon"), None),
            P(("grp", "lat", "lon")),
            P(("grp", "lat", "lon")),
            P(("grp", "lat", "lon")),
        ),
        out_specs=(P(("grp", "ch"), "lat", "lon"), P(("grp", "lat", "lon"), "ch", None)),
        check_vma=False,
    )
```

time: 145 us -> 75.7 us (0.52)
  local copies, waits for them, and re-layouts: 35.9 us -> 3.52 us
  Pallas kernels: 0 us -> 25.4 us
  waiting for transfers between devices: 24.5 us -> 8.99 us
  starting transfers between devices: 51.6 us -> 36.4 us
  other arithmetic: 13.2 us -> 0 us
  blocking collectives: 10 us -> 0 us
  matrix products: 7.13 us -> 0 us
    pallas_call x0 -> x5, Pallas kernels: none -> 25.4 us  [the longest x1 11.5 us: body(): call(forward_kernel, (shape((rows + 2, wide, c), F32), shape((rows, width...]
    gather x54 -> x0, local copies, waits for them, and re-layouts: 23.4 us -> none
    all_to_all x6 -> x2, starting transfers between devices: 26.2 us -> 10.7 us  [the longest x1 6.23 us: body(): lax.all_to_all(chunk, 'lat', split_axis=0, concat_axis=0, tiled=True)]
    ppermute x16 -> x12, waiting for transfers between devices: 20.3 us -> 8.98 us  [the longest x10 7.59 us: shifted(): return lax.ppermute(value, ('lat', 'lon'), pairs)]
    all_gather x4 -> x0, blocking collectives: 10 us -> none  [convolve(): lax.all_gather(padded, 'ch', axis=0, tiled=True)]
    dot_general x14 -> x0, matrix products: 7.13 us -> none  [the longest x12 5.9 us: apply_taps(): jnp.einsum('oi,ihw->ohw', row_kernel, stacked, preferred_element_type=jnp...]
    unnamed x5 -> x0, other arithmetic: 6.44 us -> none
    slice x14 -> x0, local copies, waits for them, and re-layouts: 6.35 us -> none  [the longest x4 4.62 us: apply_taps(): padded[:, tap_row:tap_row + grid_rows, tap_col:tap_col + grid_cols]]
  transfers between devices with their start and end apart: 22 -> 14, of which waited for: 13 -> 4; matrix products, arithmetic and copies ran while one was open for 28% -> 0% of each run, Pallas kernels for 0% -> 13%
where the time goes in v1:
time: 75.7 us; the launch traced here: 75.2 us
  starting transfers between devices  36.4 us (48%)
  Pallas kernels  25.4 us (34%)
  waiting for transfers between devices  8.99 us (12%)
  local copies, waits for them, and re-layouts  3.52 us (5%)
  between operations  0.81 us (1%)
    ppermute x10, starting transfers between devices, shifted(): return lax.ppermute(value, ('lat', 'lon'), pairs)  25.1 us
    pallas_call x1, Pallas kernels, body(): call(forward_kernel, (shape((rows + 2, wide, c), F32), shape((rows, width...  11.5 us
    ppermute x10, waiting for transfers between devices, shifted(): return lax.ppermute(value, ('lat', 'lon'), pairs)  7.59 us
    pallas_call x1, Pallas kernels, body(): call(backward_kernel, shape((half, rows, width), F32), 0, 10, [VMEM((rows...  6.44 us
    all_to_all x1, starting transfers between devices, body(): lax.all_to_all(chunk, 'lat', split_axis=0, concat_axis=0, tiled=True)  6.23 us
    all_to_all x1, starting transfers between devices, body(): back = lax.all_to_all(inn, 'lat', split_axis=0, concat_axis=0, tiled=True)  4.45 us
    unnamed x28, local copies, waits for them, and re-layouts  3.52 us
    pallas_call x1, Pallas kernels, body(): call(weights_kernel, (shape((4 * c, 6 * c), BF16),) * 4, 0, 2, [], 'weigh...  3.12 us
  transfers between devices with their start and end apart: 14, of which 4 were waited for; matrix products, arithmetic and copies ran while one was open for 0% of the time, Pallas kernels for 13%

profile of v1, /device:TPU:0, one launch (start us, length us, event | category | flops | bytes accessed | tf_op | source)
XLA Modules:
  0.0 75.2 jit_solution(16400342955529190945)
XLA Ops:
  0.6 0.6 collective-permute-start
  1.2 0.1 collective-permute-start.1
  1.3 1.4 %collective-permute-done.1.other_obs_ref = bf16[4,64,128]{2,1,0:T(8,128)(2,1)S(1)} collective-permute-done((bf16[4,64,128]{2,1,0:T(8,128)(2,1)}, bf16[4,64,128]{2,1,0:T(8,128)(2,1)S(1)}, u32[]{:S(2)}, u32[]{:S(2)}) %collective-permute-start.1) | collective-permute-done | bytes 65568 | tf_op jit(solution)/shard_map/ppermute | solution.py:375
  2.7 0.0 copy-start.7
  2.7 0.0 collective-permute-done.other_ref
  2.7 0.6 copy-done.7
  3.3 0.0 copy-start.2
  3.3 0.7 copy-done.2
  4.0 2.8 %prep.1 = (bf16[8,256,128]{2,1,0:T(8,128)(2,1)}, bf16[2,256,128]{2,1,0:T(8,128)(2,1)}, bf16[2,256,128]{2,1,0:T(8,128)(2,1)}, bf16[8,16,128]{2,1,0:T(8,128)(2,1)}...) custom-call(s32[4]{0:T(128)} %dest_ref.3, s32[4]{0:T(128)} %row_ref.1, ...), custom_call_target="tpu_custom_call" | custom-call | tf_op jit(solution)/shard_map/prep/pallas_call | solution.py:379
  6.8 6.2 %all-to-all-start = ((bf16[8,272,128]{2,1,0:T(8,128)(2,1)}), bf16[8,272,128]{2,1,0:T(8,128)(2,1)S(1)}, u32[]{:S(2)}, u32[]{:S(2)}) async-start(bf16[8,272,128]{2,1,0:T(8,128)(2,1)} %get-tuple-element.30), calls=%async_computation | async-start | bytes 1114112 | tf_op jit(solution)/shard_map/all_to_all | solution.py:387
  13.0 3.9 %collective-permute-start.3 = (bf16[2,256,128]{2,1,0:T(8,128)(2,1)}, bf16[2,256,128]{2,1,0:T(8,128)(2,1)S(1)}, u32[]{:S(2)}, u32[]{:S(2)}) collective-permute-start(bf16[2,256,128]{2,1,0:T(8,128)(2,1)} %get-tuple-element.24), channel_id=1, source_target_pairs={{0,4},{2,6},{4,8},{6,10},{8,12},{10,14},{1,5},{3,7},{5,9},{7,11},{... | collective-permute-start | bytes 393224 | tf_op jit(solution)/shard_map/ppermute | solution.py:320
  16.9 1.3 %collective-permute-start.5 = (bf16[2,256,128]{2,1,0:T(8,128)(2,1)}, bf16[2,256,128]{2,1,0:T(8,128)(2,1)S(1)}, u32[]{:S(2)}, u32[]{:S(2)}) collective-permute-start(bf16[2,256,128]{2,1,0:T(8,128)(2,1)} %get-tuple-element.26), channel_id=1, source_target_pairs={{4,0},{6,2},{8,4},{10,6},{12,8},{14,10},{5,1},{7,3},{9,5},{11,7},{... | collective-permute-start | bytes 393224 | tf_op jit(solution)/shard_map/ppermute | solution.py:320
  18.2 1.6 %collective-permute-start.2 = (bf16[8,16,128]{2,1,0:T(8,128)(2,1)}, bf16[8,16,128]{2,1,0:T(8,128)(2,1)S(1)}, u32[]{:S(2)}, u32[]{:S(2)}) collective-permute-start(bf16[8,16,128]{2,1,0:T(8,128)(2,1)} %get-tuple-element.23), channel_id=1, source_target_pairs={{0,2},{2,0},{4,6},{6,4},{8,10},{10,8},{12,14},{14,12},{1,3},{3,1},... | collective-permute-start | bytes 98312 | tf_op jit(solution)/shard_map/ppermute | solution.py:320
  19.8 4.5 %collective-permute-start.4 = (bf16[2,16,128]{2,1,0:T(8,128)(2,1)}, bf16[2,16,128]{2,1,0:T(8,128)(2,1)S(1)}, u32[]{:S(2)}, u32[]{:S(2)}) collective-permute-start(bf16[2,16,128]{2,1,0:T(8,128)(2,1)} %get-tuple-element.25), channel_id=1, source_target_pairs={{0,6},{2,4},{4,10},{6,8},{8,14},{10,12},{1,7},{3,5},{5,11},{7,9},{... | collective-permute-start | bytes 24584 | tf_op jit(solution)/shard_map/ppermute | solution.py:320
  24.3 1.3 %collective-permute-start.6 = (bf16[2,16,128]{2,1,0:T(8,128)(2,1)}, bf16[2,16,128]{2,1,0:T(8,128)(2,1)S(1)}, u32[]{:S(2)}, u32[]{:S(2)}) collective-permute-start(bf16[2,16,128]{2,1,0:T(8,128)(2,1)} %get-tuple-element.27), channel_id=1, source_target_pairs={{4,2},{6,0},{8,6},{10,4},{12,10},{14,8},{5,3},{7,1},{9,7},{11,5},{... | collective-permute-start | bytes 24584 | tf_op jit(solution)/shard_map/ppermute | solution.py:320
  25.6 3.1 %weights.1 = (bf16[512,768]{1,0:T(8,128)(2,1)}, bf16[512,768]{1,0:T(8,128)(2,1)}, bf16[512,768]{1,0:T(8,128)(2,1)}, bf16[512,768]{1,0:T(8,128)(2,1)}) custom-call(bf16[3,3,128,128]{3,2,1,0:T(8,128)(2,1)} %kin_ref.1, bf16[3,3,128,128]{3,2,1,0:T(8,128)(2,1)} %kout_ref.1), custom_call_target="tpu_custom_call" | custom-call | tf_op jit(solution)/shard_map/weights/pallas_call | solution.py:376
  28.7 0.0 collective-permute-done.4.up_tail_ref
  28.7 0.0 copy-start.10
  28.7 2.2 %collective-permute-done.6.down_tail_ref = bf16[2,16,128]{2,1,0:T(8,128)(2,1)S(1)} collective-permute-done((bf16[2,16,128]{2,1,0:T(8,128)(2,1)}, bf16[2,16,128]{2,1,0:T(8,128)(2,1)S(1)}, u32[]{:S(2)}, u32[]{:S(2)}) %collective-permute-start.6) | collective-permute-done | bytes 8224 | tf_op jit(solution)/shard_map/ppermute | solution.py:320
  30.9 0.0 copy-start.11
  30.9 0.0 collective-permute-done.2.tail_ref
  31.0 0.0 copy-start.8
  31.0 0.0 collective-permute-done.3.up_ref
  31.0 0.0 copy-start.3
  31.0 0.0 collective-permute-done.5.down_ref
  31.0 0.0 copy-start.4
  31.0 0.0 all-to-all-done.block_ref
  31.0 0.0 copy-start
  31.0 0.0 copy-done.10
  31.0 0.5 copy-done.11
  31.5 0.0 copy-done.8
  31.6 0.0 copy-done.3
  31.6 0.0 copy-done.4
  31.6 0.2 copy-done
  31.9 11.5 %forward.1 = (f32[10,272,128]{2,1,0:T(8,128)}, f32[8,256,128]{2,1,0:T(8,128)}, bf16[8,256,128]{2,1,0:T(8,128)(2,1)}, bf16[2,256,128]{2,1,0:T(8,128)(2,1)}, bf16[...) custom-call(bf16[8,256,128]{2,1,0:T(8,128)(2,1)} %get-tuple-element., ...), custom_call_target="tpu_custom_call" | custom-call | tf_op jit(solution)/shard_map/forward/pallas_call | solution.py:389
  43.3 4.5 %all-to-all-start.1 = ((bf16[8,64,128]{2,1,0:T(8,128)(2,1)}), bf16[8,64,128]{2,1,0:T(8,128)(2,1)S(1)}, u32[]{:S(2)}, u32[]{:S(2)}) async-start(bf16[8,64,128]{2,1,0:T(8,128)(2,1)} %get-tuple-element.41), calls=%async_computation.1 | async-start | bytes 262144 | tf_op jit(solution)/shard_map/all_to_all | solution.py:409
  47.8 3.9 %collective-permute-start.8 = (bf16[2,256,128]{2,1,0:T(8,128)(2,1)}, bf16[2,256,128]{2,1,0:T(8,128)(2,1)S(1)}, u32[]{:S(2)}, u32[]{:S(2)}) collective-permute-start(bf16[2,256,128]{2,1,0:T(8,128)(2,1)} %get-tuple-element.33), channel_id=1, source_target_pairs={{0,4},{2,6},{4,8},{6,10},{8,12},{10,14},{1,5},{3,7},{5,9},{7,11},{... | collective-permute-start | bytes 393224 | tf_op jit(solution)/shard_map/ppermute | solution.py:320
  51.7 1.3 %collective-permute-start.10 = (bf16[2,256,128]{2,1,0:T(8,128)(2,1)}, bf16[2,256,128]{2,1,0:T(8,128)(2,1)S(1)}, u32[]{:S(2)}, u32[]{:S(2)}) collective-permute-start(bf16[2,256,128]{2,1,0:T(8,128)(2,1)} %get-tuple-element.35), channel_id=1, source_target_pairs={{4,0},{6,2},{8,4},{10,6},{12,8},{14,10},{5,1},{7,3},{9,5},{11,7},{... | collective-permute-start | bytes 393224 | tf_op jit(solution)/shard_map/ppermute | solution.py:320
  53.0 0.7 collective-permute-start.7
  53.8 5.3 %collective-permute-start.9 = (bf16[2,16,128]{2,1,0:T(8,128)(2,1)}, bf16[2,16,128]{2,1,0:T(8,128)(2,1)S(1)}, u32[]{:S(2)}, u32[]{:S(2)}) collective-permute-start(bf16[2,16,128]{2,1,0:T(8,128)(2,1)} %get-tuple-element.34), channel_id=1, source_target_pairs={{0,6},{2,4},{4,10},{6,8},{8,14},{10,12},{1,7},{3,5},{5,11},{7,9},{... | collective-permute-start | bytes 24584 | tf_op jit(solution)/shard_map/ppermute | solution.py:320
  59.1 1.3 %collective-permute-start.11 = (bf16[2,16,128]{2,1,0:T(8,128)(2,1)}, bf16[2,16,128]{2,1,0:T(8,128)(2,1)S(1)}, u32[]{:S(2)}, u32[]{:S(2)}) collective-permute-start(bf16[2,16,128]{2,1,0:T(8,128)(2,1)} %get-tuple-element.36), channel_id=1, source_target_pairs={{4,2},{6,0},{8,6},{10,4},{12,10},{14,8},{5,3},{7,1},{9,7},{11,5},{... | collective-permute-start | bytes 24584 | tf_op jit(solution)/shard_map/ppermute | solution.py:320
  60.4 0.3 collective-permute-done.9.up_tail_ref
  60.7 0.0 copy-start.12
  60.7 5.1 %collective-permute-done.11.down_tail_ref = bf16[2,16,128]{2,1,0:T(8,128)(2,1)S(1)} collective-permute-done((bf16[2,16,128]{2,1,0:T(8,128)(2,1)}, bf16[2,16,128]{2,1,0:T(8,128)(2,1)S(1)}, u32[]{:S(2)}, u32[]{:S(2)}) %collective-permute-start.11) | collective-permute-done | bytes 8224 | tf_op jit(solution)/shard_map/ppermute | solution.py:320
  65.7 0.0 copy-start.13
  65.8 0.0 collective-permute-done.7.tail_ref
  65.8 0.0 copy-start.9
  65.8 0.0 collective-permute-done.8.up_ref
  65.8 0.0 copy-start.5
  65.8 0.0 collective-permute-done.10.down_ref
  65.8 0.0 copy-start.6
  65.8 0.0 copy-done.12
  65.8 0.5 copy-done.13
  66.3 0.0 copy-done.9
  66.4 0.0 copy-done.5
  66.4 0.0 copy-done.6
  66.5 6.4 %backward.1 = f32[64,8,256]{2,1,0:T(8,128)} custom-call(bf16[8,256,128]{2,1,0:T(8,128)(2,1)} %get-tuple-element.31.x_ref, bf16[8,16,128]{2,1,0:T(8,128)(2,1)} %copy-done.9, bf16[2,256,128]{2,1,0:T(8,128)(2,1)} %copy-done.5, bf16[2,16,128]{2,1,0:T(8,128)(2,1)} %copy-done.12, bf16[2,256,128]{2,1,0:T(8,128)(2,1)} %copy-done.6, bf16[2,16,128]{2,1,0:T(8,128)(2,1)} %copy-done.13, ...), custom_call_target="tpu_custom_call" | custom-call | tf_op jit(solution)/shard_map/backward/pallas_call | solution.py:410
  72.9 0.0 all-to-all-done.1.back_ref
  72.9 0.0 copy-start.1
  72.9 0.6 copy-done.1
  73.6 1.6 %innovation.1 = bf16[4,64,128]{2,1,0:T(8,128)(2,1)} custom-call(s32[4]{0:T(128)} %dest_ref.3, bf16[8,64,128]{2,1,0:T(8,128)(2,1)} %copy-done.1), custom_call_target="tpu_custom_call" | custom-call | tf_op jit(solution)/shard_map/innovation/pallas_call | solution.py:422
Async XLA Ops:
  0.6 2.0 %collective-permute-start = (bf16[64,8,256]{2,1,0:T(8,128)(2,1)}, bf16[64,8,256]{2,1,0:T(8,128)(2,1)S(1)}, u32[]{:S(2)}, u32[]{:S(2)}) collective-permute-start(bf16[64,8,256]{2,1,0:T(8,128)(2,1)} %own_ref.1), channel_id=1, source_target_pairs={{0,1},{1,0},{2,3},{3,2},{4,5},{5,4},{6,7},{7,6},{8,9},{9,8},{10,11... | collective-permute-start | bytes 786440 | tf_op jit(solution)/shard_map/ppermute | solution.py:374
  1.2 1.5 %collective-permute-start.1 = (bf16[4,64,128]{2,1,0:T(8,128)(2,1)}, bf16[4,64,128]{2,1,0:T(8,128)(2,1)S(1)}, u32[]{:S(2)}, u32[]{:S(2)}) collective-permute-start(bf16[4,64,128]{2,1,0:T(8,128)(2,1)} %own_obs_ref.1), channel_id=1, source_target_pairs={{0,1},{1,0},{2,3},{3,2},{4,5},{5,4},{6,7},{7,6},{8,9},{9,8},{10,11... | collective-permute-start | bytes 196616 | tf_op jit(solution)/shard_map/ppermute | solution.py:375
  2.7 0.6 copy-start.7
  3.3 0.7 copy-start.2
  6.8 24.2 %all-to-all-start = ((bf16[8,272,128]{2,1,0:T(8,128)(2,1)}), bf16[8,272,128]{2,1,0:T(8,128)(2,1)S(1)}, u32[]{:S(2)}, u32[]{:S(2)}) async-start(bf16[8,272,128]{2,1,0:T(8,128)(2,1)} %get-tuple-element.30), calls=%async_computation | async-start | bytes 1114112 | tf_op jit(solution)/shard_map/all_to_all | solution.py:387
  13.0 18.0 %collective-permute-start.3 = (bf16[2,256,128]{2,1,0:T(8,128)(2,1)}, bf16[2,256,128]{2,1,0:T(8,128)(2,1)S(1)}, u32[]{:S(2)}, u32[]{:S(2)}) collective-permute-start(bf16[2,256,128]{2,1,0:T(8,128)(2,1)} %get-tuple-element.24), channel_id=1, source_target_pairs={{0,4},{2,6},{4,8},{6,10},{8,12},{10,14},{1,5},{3,7},{5,9},{7,11},{... | collective-permute-start | bytes 393224 | tf_op jit(solution)/shard_map/ppermute | solution.py:320
  16.9 14.0 %collective-permute-start.5 = (bf16[2,256,128]{2,1,0:T(8,128)(2,1)}, bf16[2,256,128]{2,1,0:T(8,128)(2,1)S(1)}, u32[]{:S(2)}, u32[]{:S(2)}) collective-permute-start(bf16[2,256,128]{2,1,0:T(8,128)(2,1)} %get-tuple-element.26), channel_id=1, source_target_pairs={{4,0},{6,2},{8,4},{10,6},{12,8},{14,10},{5,1},{7,3},{9,5},{11,7},{... | collective-permute-start | bytes 393224 | tf_op jit(solution)/shard_map/ppermute | solution.py:320
  18.2 12.7 %collective-permute-start.2 = (bf16[8,16,128]{2,1,0:T(8,128)(2,1)}, bf16[8,16,128]{2,1,0:T(8,128)(2,1)S(1)}, u32[]{:S(2)}, u32[]{:S(2)}) collective-permute-start(bf16[8,16,128]{2,1,0:T(8,128)(2,1)} %get-tuple-element.23), channel_id=1, source_target_pairs={{0,2},{2,0},{4,6},{6,4},{8,10},{10,8},{12,14},{14,12},{1,3},{3,1},... | collective-permute-start | bytes 98312 | tf_op jit(solution)/shard_map/ppermute | solution.py:320
  19.8 8.9 %collective-permute-start.4 = (bf16[2,16,128]{2,1,0:T(8,128)(2,1)}, bf16[2,16,128]{2,1,0:T(8,128)(2,1)S(1)}, u32[]{:S(2)}, u32[]{:S(2)}) collective-permute-start(bf16[2,16,128]{2,1,0:T(8,128)(2,1)} %get-tuple-element.25), channel_id=1, source_target_pairs={{0,6},{2,4},{4,10},{6,8},{8,14},{10,12},{1,7},{3,5},{5,11},{7,9},{... | collective-permute-start | bytes 24584 | tf_op jit(solution)/shard_map/ppermute | solution.py:320
  24.3 6.7 %collective-permute-start.6 = (bf16[2,16,128]{2,1,0:T(8,128)(2,1)}, bf16[2,16,128]{2,1,0:T(8,128)(2,1)S(1)}, u32[]{:S(2)}, u32[]{:S(2)}) collective-permute-start(bf16[2,16,128]{2,1,0:T(8,128)(2,1)} %get-tuple-element.27), channel_id=1, source_target_pairs={{4,2},{6,0},{8,6},{10,4},{12,10},{14,8},{5,3},{7,1},{9,7},{11,5},{... | collective-permute-start | bytes 24584 | tf_op jit(solution)/shard_map/ppermute | solution.py:320
  28.7 2.3 %copy-start.10 = (bf16[2,16,128]{2,1,0:T(8,128)(2,1)}, bf16[2,16,128]{2,1,0:T(8,128)(2,1)S(1)}, u32[]{:S(2)}) copy-start(bf16[2,16,128]{2,1,0:T(8,128)(2,1)S(1)} %collective-permute-done.4.up_tail_ref) | copy-start | bytes 24580
  30.9 0.6 copy-start.11
  31.0 0.6 copy-start.8
  31.0 0.6 copy-start.3
  31.0 0.7 copy-start.4
  31.0 0.9 %copy-start = (bf16[8,272,128]{2,1,0:T(8,128)(2,1)}, bf16[8,272,128]{2,1,0:T(8,128)(2,1)S(1)}, u32[]{:S(2)}) copy-start(bf16[8,272,128]{2,1,0:T(8,128)(2,1)S(1)} %all-to-all-done.block_ref) | copy-start | bytes 1671172
  43.3 29.6 %all-to-all-start.1 = ((bf16[8,64,128]{2,1,0:T(8,128)(2,1)}), bf16[8,64,128]{2,1,0:T(8,128)(2,1)S(1)}, u32[]{:S(2)}, u32[]{:S(2)}) async-start(bf16[8,64,128]{2,1,0:T(8,128)(2,1)} %get-tuple-element.41), calls=%async_computation.1 | async-start | bytes 262144 | tf_op jit(solution)/shard_map/all_to_all | solution.py:409
  47.8 18.0 %collective-permute-start.8 = (bf16[2,256,128]{2,1,0:T(8,128)(2,1)}, bf16[2,256,128]{2,1,0:T(8,128)(2,1)S(1)}, u32[]{:S(2)}, u32[]{:S(2)}) collective-permute-start(bf16[2,256,128]{2,1,0:T(8,128)(2,1)} %get-tuple-element.33), channel_id=1, source_target_pairs={{0,4},{2,6},{4,8},{6,10},{8,12},{10,14},{1,5},{3,7},{5,9},{7,11},{... | collective-permute-start | bytes 393224 | tf_op jit(solution)/shard_map/ppermute | solution.py:320
  51.7 14.0 %collective-permute-start.10 = (bf16[2,256,128]{2,1,0:T(8,128)(2,1)}, bf16[2,256,128]{2,1,0:T(8,128)(2,1)S(1)}, u32[]{:S(2)}, u32[]{:S(2)}) collective-permute-start(bf16[2,256,128]{2,1,0:T(8,128)(2,1)} %get-tuple-element.35), channel_id=1, source_target_pairs={{4,0},{6,2},{8,4},{10,6},{12,8},{14,10},{5,1},{7,3},{9,5},{11,7},{... | collective-permute-start | bytes 393224 | tf_op jit(solution)/shard_map/ppermute | solution.py:320
  53.0 12.7 %collective-permute-start.7 = (bf16[8,16,128]{2,1,0:T(8,128)(2,1)}, bf16[8,16,128]{2,1,0:T(8,128)(2,1)S(1)}, u32[]{:S(2)}, u32[]{:S(2)}) collective-permute-start(bf16[8,16,128]{2,1,0:T(8,128)(2,1)} %get-tuple-element.32), channel_id=1, source_target_pairs={{0,2},{2,0},{4,6},{6,4},{8,10},{10,8},{12,14},{14,12},{1,3},{3,1},... | collective-permute-start | bytes 98312 | tf_op jit(solution)/shard_map/ppermute | solution.py:320
  53.8 6.9 %collective-permute-start.9 = (bf16[2,16,128]{2,1,0:T(8,128)(2,1)}, bf16[2,16,128]{2,1,0:T(8,128)(2,1)S(1)}, u32[]{:S(2)}, u32[]{:S(2)}) collective-permute-start(bf16[2,16,128]{2,1,0:T(8,128)(2,1)} %get-tuple-element.34), channel_id=1, source_target_pairs={{0,6},{2,4},{4,10},{6,8},{8,14},{10,12},{1,7},{3,5},{5,11},{7,9},{... | collective-permute-start | bytes 24584 | tf_op jit(solution)/shard_map/ppermute | solution.py:320
  59.1 6.7 %collective-permute-start.11 = (bf16[2,16,128]{2,1,0:T(8,128)(2,1)}, bf16[2,16,128]{2,1,0:T(8,128)(2,1)S(1)}, u32[]{:S(2)}, u32[]{:S(2)}) collective-permute-start(bf16[2,16,128]{2,1,0:T(8,128)(2,1)} %get-tuple-element.36), channel_id=1, source_target_pairs={{4,2},{6,0},{8,6},{10,4},{12,10},{14,8},{5,3},{7,1},{9,7},{11,5},{... | collective-permute-start | bytes 24584 | tf_op jit(solution)/shard_map/ppermute | solution.py:320
  60.7 5.1 %copy-start.12 = (bf16[2,16,128]{2,1,0:T(8,128)(2,1)}, bf16[2,16,128]{2,1,0:T(8,128)(2,1)S(1)}, u32[]{:S(2)}) copy-start(bf16[2,16,128]{2,1,0:T(8,128)(2,1)S(1)} %collective-permute-done.9.up_tail_ref) | copy-start | bytes 24580
  65.7 0.6 copy-start.13
  65.8 0.6 copy-start.9
  65.8 0.7 copy-start.5
  65.8 0.7 copy-start.6
  72.9 0.7 copy-start.1

commit v2 on v1

v2 whole, which is shorter than its diff:
```python
import functools

import jax
import jax.numpy as jnp
from jax import lax
from jax.experimental import pallas as pl
from jax.experimental.pallas import tpu as pltpu
from jax.sharding import PartitionSpec as P

PH = 4
PW = 32
CAP = 2
TAIL = 16
META = 16

keep_rate = 0.6
blend_rate = 0.4
guide_rate = 0.3

F32 = jnp.float32
BF16 = jnp.bfloat16
VMEM = pltpu.VMEM
SMEM = pltpu.SMEM
HBM = pltpu.MemorySpace.HBM
OUT = "out"


def call(kernel, outs, ins, scratch, name):
    near = lambda v, space: v if space == OUT else space(v.shape, v.dtype)
    spec = lambda space: pl.BlockSpec(memory_space=VMEM if space == OUT else space)
    run = pl.pallas_call(
        kernel,
        out_shape=[near(v, space) for v, space in outs],
        in_specs=[spec(space) for space in ins],
        out_specs=[spec(space) for _, space in outs],
        scratch_shapes=scratch,
        compiler_params=pltpu.CompilerParams(vmem_limit_bytes=24 * 1024 * 1024),
        name=name,
    )

    def apply(*args):
        return run(
            *(pltpu.with_memory_space_constraint(a, space) if space in (VMEM, HBM) else a for a, space in zip(args, ins))
        )

    return apply


def place_taps(w_ref, tap_of):
    c = w_ref.shape[0] // 4
    for b in range(3):
        for a in range(3):
            tap = tap_of(a, b)
            for row in range(2):
                at = (2 * b + row) * c
                w_ref[(a + row) * c : (a + row + 1) * c, at : at + c] = tap
        w_ref[3 * c : 4 * c, 2 * b * c : (2 * b + 1) * c] = jnp.zeros((c, c), BF16)
        w_ref[0:c, (2 * b + 1) * c : (2 * b + 2) * c] = jnp.zeros((c, c), BF16)


def weights_kernel(kin_ref, kout_ref, w1_ref, w2_ref):
    for w_ref, k_ref in ((w1_ref, kin_ref), (w2_ref, kout_ref)):
        place_taps(w_ref, lambda a, b: k_ref[a, b].astype(F32).T.astype(BF16))


def tail_of(row_ref, width):
    lane_rows = lax.broadcasted_iota(jnp.int32, (TAIL, row_ref.shape[-1]), 0)
    first = row_ref[0:TAIL, :].astype(F32)
    last = row_ref[width - TAIL : width, :].astype(F32)
    zero = jnp.zeros_like(first)
    return jnp.where(lane_rows < 2, first, jnp.where(lane_rows >= TAIL - 2, last, zero)).astype(BF16)


def write_edges(x_ref, edge_ref, tail_ref, edge_tail_ref):
    rows, width = x_ref.shape[0], x_ref.shape[1]
    first = lax.axis_index("ch") * (rows - 2)
    for h in range(rows):
        tail_ref[h] = tail_of(x_ref.at[h], width)
    for i in range(2):
        edge_ref[i] = x_ref[first + i]
        edge_tail_ref[i] = tail_ref[first + i]


def prep_kernel(
    dest_ref,
    row_ref,
    col_ref,
    own_ref,
    other_ref,
    own_obs_ref,
    other_obs_ref,
    weight_ref,
    precision_ref,
    x_ref,
    edge_ref,
    tail_ref,
    edge_tail_ref,
    chunk_ref,
    flat_ref,
    scale_ref,
):
    core = lax.axis_index("ch")
    half, rows, width = own_ref.shape
    obs = weight_ref.shape[1]
    cells = weight_ref.shape[2]
    blocks = weight_ref.shape[0]

    def place(ref, first):
        for part in range(width // 128):
            piece = ref[:, :, part * 128 : (part + 1) * 128].astype(F32)
            flat_ref[part, pl.ds(pl.multiple_of(first * rows, 8), half * rows), :] = piece.reshape(half * rows, 128)

    place(own_ref, core * half)
    place(other_ref, (1 - core) * half)
    for h in range(rows):
        for part in range(width // 128):
            plane = flat_ref[part, pl.ds(h, 2 * half, stride=rows), :]
            x_ref[h, part * 128 : (part + 1) * 128, :] = plane.T.astype(BF16)
    write_edges(x_ref, edge_ref, tail_ref, edge_tail_ref)

    def clear(slot, _):
        chunk_ref[slot] = jnp.zeros(chunk_ref.shape[1:], BF16)
        return 0

    lax.fori_loop(0, chunk_ref.shape[0], clear, 0)
    scale_ref[...] = precision_ref[...].astype(F32)
    meta_rows = lax.broadcasted_iota(jnp.int32, (META, obs), 0)

    def pack(b, _):
        dest = dest_ref[b]
        rank = lax.fori_loop(0, b, lambda j, n: n + (dest_ref[j] == dest).astype(jnp.int32), 0)

        @pl.when(rank == core)
        def _():
            fill(b, dest)

        return 0

    def fill(b, slot):
        chunk_ref[slot, 0:obs, :] = weight_ref[b]
        chunk_ref[slot, pl.ds(pl.multiple_of(obs + core * half, 16), half), :] = own_obs_ref[b]
        chunk_ref[slot, pl.ds(pl.multiple_of(obs + (1 - core) * half, 16), half), :] = other_obs_ref[b]
        row = row_ref[b].astype(F32)
        high = lax.div(col_ref[b], 16).astype(F32)
        low = lax.rem(col_ref[b], 16).astype(F32)
        meta = jnp.where(
            meta_rows == 0,
            jnp.broadcast_to(scale_ref[pl.ds(b, 1), :], (META, obs)),
            jnp.where(meta_rows == 1, row, jnp.where(meta_rows == 2, high, low)),
        )
        chunk_ref[slot, obs + 2 * half : obs + 2 * half + META, :] = meta.astype(BF16)

    lax.fori_loop(0, blocks, pack, 0)


def fill_extended(ext_ref, x_ref, tail_ref, mine_ref, mine_tail_ref, other_ref, other_tail_ref):
    rows, width = x_ref.shape[0], x_ref.shape[1]
    core = lax.axis_index("ch")
    for i in range(2):
        mine = core * (rows + 2) + i
        other = (1 - core) * (rows + 2) + i
        ext_ref[mine, 0:width, :] = mine_ref[i]
        ext_ref[mine, width : width + TAIL, :] = mine_tail_ref[i]
        ext_ref[other, 0:width, :] = other_ref[i]
        ext_ref[other, width : width + TAIL, :] = other_tail_ref[i]
    for h in range(rows):
        ext_ref[h + 2, 0:width, :] = x_ref[h]
        ext_ref[h + 2, width : width + TAIL, :] = tail_ref[h]


def row_pair(src_ref, w_ref, first):
    c = src_ref.shape[-1]
    wide = src_ref.shape[1]
    lhs = jnp.concatenate([src_ref[first + k] for k in range(4)], axis=1)
    y = jnp.dot(lhs, w_ref[...], preferred_element_type=F32)
    out = []
    for row in range(2):
        left, mid, right = (y[:, (2 * b + row) * c : (2 * b + row + 1) * c] for b in range(3))
        out.append(pltpu.roll(left, 1, 0) + mid + pltpu.roll(right, wide - 1, 0))
    return out


def inside(ext_row, ext_rows):
    at = lax.axis_index("lat")
    last = lax.axis_size("lat") - 1
    return ((ext_row > 0) | (at > 0)) & ((ext_row < ext_rows - 1) | (at < last))


def forward_kernel(
    x_ref,
    tail_ref,
    mine_ref,
    mine_tail_ref,
    other_ref,
    other_tail_ref,
    w1_ref,
    w2_ref,
    bias_ref,
    block_ref,
    other_block_ref,
    slope_out_ref,
    base_ref,
    g_ref,
    edge_ref,
    gtail_ref,
    edge_tail_ref,
    inn_ref,
    ext_ref,
    hidden_ref,
    den_ref,
    field_ref,
    slope_ref,
    save_sem,
):
    core = lax.axis_index("ch")
    rows, width, c = x_ref.shape
    half = inn_ref.shape[1]
    sources, obs = block_ref.shape[0], block_ref.shape[2]
    fill_extended(ext_ref, x_ref, tail_ref, mine_ref, mine_tail_ref, other_ref, other_tail_ref)
    bias = bias_ref[...]

    def first_conv(g, _):
        for i, y in enumerate(row_pair(ext_ref, w1_ref, 2 * g)):
            r = 2 * g + i
            pre = y + bias
            s = 1.0 / (1.0 + jnp.exp(-pre))
            slope_ref[r] = s * (1.0 + pre * (1.0 - s))
            hidden = pre * s
            hidden_ref[r] = jnp.where(inside(r, rows + 2), hidden, 0.0).astype(BF16)
        return 0

    lax.fori_loop(0, (rows + 2) // 2, first_conv, 0)
    save = pltpu.make_async_copy(slope_ref, slope_out_ref, save_sem)
    save.start()

    def second_conv(g, _):
        for i, y in enumerate(row_pair(hidden_ref, w2_ref, 2 * g)):
            r = 2 * g + i
            noisy = x_ref[r].astype(F32)
            den = (noisy + y[0:width, :]).astype(BF16).astype(F32)
            den_ref[r] = den
            base_ref[r] = keep_rate * noisy + blend_rate * den
            field_ref[r] = jnp.zeros((width, c), F32)
        return 0

    lax.fori_loop(0, rows // 2, second_conv, 0)

    def observe(source, cap):
        slot = source * CAP + cap

        def read(first, count):
            at = slice(first, first + count)
            return jnp.where(core == cap, block_ref[source, at, :], other_block_ref[source, at, :])

        meta = read(obs + c, META).astype(F32)
        row = jnp.max(meta[1:2, :]).astype(jnp.int32)
        col = jnp.max(meta[2:3, :]).astype(jnp.int32) * 16 + jnp.max(meta[3:4, :]).astype(jnp.int32)
        weight = read(0, obs)
        patch = jnp.concatenate([den_ref[row + i, pl.ds(col, PW), :] for i in range(PH)], axis=0)
        predicted = lax.dot_general(
            patch.T.astype(BF16), weight, (((1,), (1,)), ((), ())), preferred_element_type=F32
        )
        residual = predicted - read(obs, c).astype(F32)
        inn_ref[slot] = jnp.where(core == 0, residual[0:half], residual[half : 2 * half]).astype(BF16)
        weighted = (residual * meta[0:1, :]).astype(BF16)
        pulled = jnp.dot(weighted, weight, preferred_element_type=F32).T
        for i in range(PH):
            field_ref[row + i, pl.ds(col, PW), :] += pulled[i * PW : (i + 1) * PW, :]

    def observe_source(source, _):
        for cap in range(CAP):
            observe(source, cap)
        return 0

    lax.fori_loop(0, sources, observe_source, 0)

    for r in range(rows):
        field = field_ref[r]
        base_ref[r] -= guide_rate * field
        g_ref[r] = field.astype(BF16)
    write_edges(g_ref, edge_ref, gtail_ref, edge_tail_ref)
    save.wait()


def backward_kernel(
    x_ref,
    tail_ref,
    mine_ref,
    mine_tail_ref,
    other_ref,
    other_tail_ref,
    kin_ref,
    kout_ref,
    base_ref,
    slope_in_ref,
    next_ref,
    ext_ref,
    grad_ref,
    flat_ref,
    w3_ref,
    w4_ref,
    slope_ref,
    load_sems,
):
    core = lax.axis_index("ch")
    rows, width, c = x_ref.shape
    half = next_ref.shape[0]
    groups = (rows + 2) // 2

    def load(g):
        at = pl.ds(2 * g, 2)
        return pltpu.make_async_copy(slope_in_ref.at[at], slope_ref.at[at], load_sems.at[g])

    for g in range(groups):
        load(g).start()
    fill_extended(ext_ref, x_ref, tail_ref, mine_ref, mine_tail_ref, other_ref, other_tail_ref)
    place_taps(w3_ref, lambda a, b: kout_ref[2 - a, 2 - b])
    place_taps(w4_ref, lambda a, b: kin_ref[2 - a, 2 - b])

    for g in range(groups):
        load(g).wait()
        for i, y in enumerate(row_pair(ext_ref, w3_ref, 2 * g)):
            r = 2 * g + i
            grad = y * slope_ref[r]
            grad_ref[r] = jnp.where(inside(r, rows + 2), grad, 0.0).astype(BF16)

    for g in range(rows // 2):
        for i, y in enumerate(row_pair(grad_ref, w4_ref, 2 * g)):
            r = 2 * g + i
            out = base_ref[r] - guide_rate * y[0:width, :]
            for part in range(width // 128):
                plane = out[part * 128 : (part + 1) * 128, :].T
                own = jnp.where(core == 0, plane[0:half], plane[half : 2 * half])
                flat_ref[part, pl.ds(r, half, stride=rows), :] = own
    for part in range(width // 128):
        next_ref[:, :, part * 128 : (part + 1) * 128] = flat_ref[part].reshape(half, rows, 128)


def return_kernel(dest_ref, back_ref, inn_ref):
    def take(b, _):
        dest = dest_ref[b]
        rank = lax.fori_loop(0, b, lambda j, n: n + (dest_ref[j] == dest).astype(jnp.int32), 0)
        inn_ref[b] = back_ref[dest * CAP + rank]
        return 0

    lax.fori_loop(0, inn_ref.shape[0], take, 0)


def swapped(value):
    return lax.ppermute(value, "ch", [(0, 1), (1, 0)])


def from_row_neighbour(value, lon_step):
    lats, lons = lax.axis_size("lat"), lax.axis_size("lon")
    pairs = []
    for i in range(lats):
        for j in range(lons):
            for core, step in ((0, -1), (1, 1)):
                if 0 <= i + step < lats:
                    to = (i + step) * lons + (j + lon_step) % lons
                    pairs.append(((i * lons + j) * 2 + core, to * 2 + 1 - core))
    return lax.ppermute(value, ("lat", "lon", "ch"), pairs)


def from_lon_neighbour(value, lon_step):
    lons = lax.axis_size("lon")
    return lax.ppermute(value, "lon", [(j, (j + lon_step) % lons) for j in range(lons)])


def both_sides(move, value):
    if lax.axis_size("lon") == 2:
        return move(value, 1)
    from_right = move(value, -1)
    from_left = move(value, 1)
    at = lax.broadcasted_iota(jnp.int32, (1, TAIL, 1), 1)
    return jnp.where(at < TAIL // 2, from_right, from_left)


def exchanged(edge, tail, edge_tail, along):
    mine = from_row_neighbour(edge, 0)
    beside = both_sides(from_lon_neighbour, tail)
    mine_tail = both_sides(from_row_neighbour, edge_tail)
    *halo, along = lax.optimization_barrier((beside, mine, mine_tail, along))
    return tuple(halo), along


def shape(dims, dtype):
    return jax.ShapeDtypeStruct(dims, dtype)


def edge_shapes(rows, width, c):
    return [
        (shape((2, width, c), BF16), VMEM),
        (shape((rows, TAIL, c), BF16), VMEM),
        (shape((2, TAIL, c), BF16), VMEM),
    ]


def body(
    noisy_state,
    kernel_in,
    bias_in,
    kernel_out,
    interp_weight,
    observed,
    obs_precision,
    dest_tile,
    row_offset,
    col_offset,
):
    half, rows, width = noisy_state.shape
    c = kernel_in.shape[-1]
    obs = interp_weight.shape[1]
    lats = lax.axis_size("lat")
    slots = lats * CAP
    wide = width + TAIL
    other = swapped(noisy_state)
    other_obs = swapped(observed)
    w1, w2 = call(weights_kernel, [(shape((4 * c, 6 * c), BF16), VMEM)] * 2, [VMEM] * 2, [], "weights")(
        kernel_in, kernel_out
    )
    x, *edges, chunk = call(
        prep_kernel,
        [
            (shape((rows, width, c), BF16), VMEM),
            *edge_shapes(rows, width, c),
            (shape((lats, obs + c + META, obs), BF16), VMEM),
        ],
        [SMEM] * 3 + [VMEM] * 6,
        [VMEM((width // 128, c * rows, 128), F32), VMEM(obs_precision.shape, F32)],
        "prep",
    )(dest_tile, row_offset, col_offset, noisy_state, other, observed, other_obs, interp_weight, obs_precision)
    block = lax.all_to_all(chunk, "lat", split_axis=0, concat_axis=0, tiled=True)
    halo, block = exchanged(*edges, block)
    halo = halo + (swapped(halo[1]), swapped(halo[2]))
    slope, base, g, *edges, inn = call(
        forward_kernel,
        [
            (shape((rows + 2, wide, c), F32), HBM),
            (shape((rows, width, c), F32), VMEM),
            (shape((rows, width, c), BF16), VMEM),
            *edge_shapes(rows, width, c),
            (shape((slots, half, obs), BF16), VMEM),
        ],
        [VMEM] * 11,
        [
            VMEM((rows + 4, wide, c), BF16),
            VMEM((rows + 2, wide, c), BF16),
            VMEM((rows, width, c), F32),
            VMEM((rows, width, c), F32),
            VMEM((rows + 2, wide, c), F32),
            pltpu.SemaphoreType.DMA,
        ],
        "forward",
    )(x, *halo, w1, w2, bias_in.reshape(1, c), block, swapped(block))
    back = lax.all_to_all(inn, "lat", split_axis=0, concat_axis=0, tiled=True)
    halo, _ = exchanged(*edges, ())
    halo = halo + (swapped(halo[1]), swapped(halo[2]))
    (next_state,) = call(
        backward_kernel,
        [(shape((half, rows, width), F32), OUT)],
        [VMEM] * 9 + [HBM],
        [
            VMEM((rows + 4, wide, c), BF16),
            VMEM((rows + 2, wide, c), BF16),
            VMEM((width // 128, half * rows, 128), F32),
            VMEM((4 * c, 6 * c), BF16),
            VMEM((4 * c, 6 * c), BF16),
            VMEM((rows + 2, wide, c), F32),
            pltpu.SemaphoreType.DMA(((rows + 2) // 2,)),
        ],
        "backward",
    )(g, *halo, kernel_in, kernel_out, base, slope)
    (innovation,) = call(return_kernel, [(shape(observed.shape, BF16), OUT)], [SMEM, VMEM], [], "innovation")(
        dest_tile, back
    )
    return next_state, innovation


def solution(mesh):
    return jax.shard_map(
        body,
        mesh=mesh,
        in_specs=(
            P(("grp", "ch"), "lat", "lon"),
            P(),
            P(),
            P(),
            P(("grp", "lat", "lon"), None, None),
            P(("grp", "lat", "lon"), "ch", None),
            P(("grp", "lat", "lon"), None),
            P(("grp", "lat", "lon")),
            P(("grp", "lat", "lon")),
            P(("grp", "lat", "lon")),
        ),
        out_specs=(P(("grp", "ch"), "lat", "lon"), P(("grp", "lat", "lon"), "ch", None)),
        check_vma=False,
    )
```

time: 75.7 us -> 57.2 us (0.76)
  starting transfers between devices: 36.4 us -> 23.1 us
  Pallas kernels: 25.4 us -> 16.1 us
  waiting for transfers between devices: 8.99 us -> 11.4 us
  local copies, waits for them, and re-layouts: 3.52 us -> 5.35 us
    ppermute x12 -> x13, starting transfers between devices: 25.8 us -> 10.5 us  [the longest x7 5.83 us: swapped(): return lax.ppermute(value, 'ch', [(0, 1), (1, 0)])]
    pallas_call x5, Pallas kernels: 25.4 us -> 16.1 us  [apply(): run(*(pltpu.with_memory_space_constraint(a, space) if space in (VMEM, HBM...]
    all_to_all x1, waiting for transfers between devices: 0.01 us -> 4.91 us  [body(): lax.all_to_all(chunk, 'lat', split_axis=0, concat_axis=0, tiled=True)]
    ppermute x12 -> x13, waiting for transfers between devices: 8.98 us -> 6.46 us  [the longest x2 4.47 us: from_lon_neighbour(): lax.ppermute(value, 'lon', [(j, (j + lon_step) % lons) for j in range(lon...]
    all_to_all x1, starting transfers between devices: 4.45 us -> 6.33 us  [body(): back = lax.all_to_all(inn, 'lat', split_axis=0, concat_axis=0, tiled=True)]
    unnamed x28 -> x22, local copies, waits for them, and re-layouts: 3.52 us -> 5.35 us
  transfers between devices with their start and end apart: 14 -> 15, of which waited for: 4 -> 5; matrix products, arithmetic and copies ran while one was open for 0% -> 0% of each run, Pallas kernels for 13% -> 3%
where the time goes in v2:
time: 57.2 us; the launch traced here: 56.7 us
  starting transfers between devices  23.1 us (40%)
  Pallas kernels  16.1 us (28%)
  waiting for transfers between devices  11.4 us (20%)
  local copies, waits for them, and re-layouts  5.35 us (9%)
  between operations  0.75 us (1%)
    pallas_call x5, Pallas kernels, apply(): run(*(pltpu.with_memory_space_constraint(a, space) if space in (VMEM, HBM...  16.1 us
    all_to_all x1, starting transfers between devices, body(): back = lax.all_to_all(inn, 'lat', split_axis=0, concat_axis=0, tiled=True)  6.33 us
    all_to_all x1, starting transfers between devices, body(): lax.all_to_all(chunk, 'lat', split_axis=0, concat_axis=0, tiled=True)  6.24 us
    ppermute x7, starting transfers between devices, swapped(): return lax.ppermute(value, 'ch', [(0, 1), (1, 0)])  5.83 us
    unnamed x22, local copies, waits for them, and re-layouts  5.35 us
    all_to_all x1, waiting for transfers between devices, body(): lax.all_to_all(chunk, 'lat', split_axis=0, concat_axis=0, tiled=True)  4.91 us
    ppermute x2, waiting for transfers between devices, from_lon_neighbour(): lax.ppermute(value, 'lon', [(j, (j + lon_step) % lons) for j in range(lon...  4.47 us
    ppermute x4, starting transfers between devices, from_row_neighbour(): return lax.ppermute(value, ('lat', 'lon', 'ch'), pairs)  2.62 us
  transfers between devices with their start and end apart: 15, of which 5 were waited for; matrix products, arithmetic and copies ran while one was open for 0% of the time, Pallas kernels for 3%

profile of v2, /device:TPU:0, one launch (start us, length us, event | category | flops | bytes accessed | tf_op | source)
XLA Modules:
  0.0 56.7 jit_solution(337345584938977890)
XLA Ops:
  0.6 0.0 copy-start.1
  0.6 0.0 copy-start
  0.7 0.6 collective-permute-start
  1.2 0.1 collective-permute-start.1
  1.3 1.4 %collective-permute-done.1.other_obs_ref = bf16[4,64,128]{2,1,0:T(8,128)(2,1)S(1)} collective-permute-done((bf16[4,64,128]{2,1,0:T(8,128)(2,1)}, bf16[4,64,128]{2,1,0:T(8,128)(2,1)S(1)}, u32[]{:S(2)}, u32[]{:S(2)}) %collective-permute-start.1) | collective-permute-done | bytes 65568 | tf_op jit(solution)/shard_map/ppermute | solution.py:350
  2.7 0.0 collective-permute-done.other_ref
  2.7 0.0 copy-start.2
  2.7 0.9 %copy-done.2 = bf16[64,8,256]{2,1,0:T(8,128)(2,1)S(1)} copy-done((bf16[64,8,256]{2,1,0:T(8,128)(2,1)S(1)}, bf16[64,8,256]{2,1,0:T(8,128)(2,1)}, u32[]{:S(2)}) %copy-start.2) | copy-done | bytes 262168
  3.6 0.0 copy-start.3
  3.6 0.9 %copy-done.3 = bf16[4,128,128]{2,1,0:T(8,128)(2,1)S(1)} copy-done((bf16[4,128,128]{2,1,0:T(8,128)(2,1)S(1)}, bf16[4,128,128]{2,1,0:T(8,128)(2,1)}, u32[]{:S(2)}) %copy-start.3) | copy-done | bytes 131096
  4.5 0.0 copy-start.4
  4.5 0.8 %copy-done.4 = bf16[4,64,128]{2,1,0:T(8,128)(2,1)S(1)} copy-done((bf16[4,64,128]{2,1,0:T(8,128)(2,1)S(1)}, bf16[4,64,128]{2,1,0:T(8,128)(2,1)}, u32[]{:S(2)}) %copy-start.4) | copy-done | bytes 65560
  5.4 0.0 copy-start.5
  5.4 0.7 %copy-done.5 = s32[4]{0:T(128)S(1)} copy-done((s32[4]{0:T(128)S(1)}, s32[4]{0:T(128)}, u32[]{:S(2)}) %copy-start.5) | copy-done | bytes 40
  6.0 0.0 copy-start.7
  6.0 0.7 %copy-done.7 = bf16[4,128]{1,0:T(4,128)(2,1)S(1)} copy-done((bf16[4,128]{1,0:T(4,128)(2,1)S(1)}, bf16[4,128]{1,0:T(4,128)(2,1)}, u32[]{:S(2)}) %copy-start.7) | copy-done | bytes 1048
  6.7 0.0 copy-start.9
  6.7 0.7 %copy-done.9 = s32[4]{0:T(128)S(1)} copy-done((s32[4]{0:T(128)S(1)}, s32[4]{0:T(128)}, u32[]{:S(2)}) %copy-start.9) | copy-done | bytes 40
  7.4 0.0 copy-start.10
  7.4 0.7 %copy-done.10 = s32[4]{0:T(128)S(1)} copy-done((s32[4]{0:T(128)S(1)}, s32[4]{0:T(128)}, u32[]{:S(2)}) %copy-start.10) | copy-done | bytes 40
  8.0 0.0 copy-start.8
  8.0 1.8 %prep.1 = (bf16[8,256,128]{2,1,0:T(8,128)(2,1)S(1)}, bf16[2,256,128]{2,1,0:T(8,128)(2,1)S(1)}, bf16[8,16,128]{2,1,0:T(8,128)(2,1)S(1)}, bf16[2,16,128]{2,1,0:T(8,128)(2,1)S(1)}, bf16[4,272,128]{2,1,0:T(8,128)(2,1)}) custom-call(s32[4]{0:T(128)S(1)} %copy-done.5, s32[4]{0:T(128)S(1)} %copy-done.9, s32[4]{0:T(128)S(1)} %copy-done.10, ...), custom_call_target="tpu_custom_call" | custom-call | tf_op jit(solution)/shard_map/prep/pallas_call | solution.py:42
  9.8 6.2 %all-to-all-start = ((bf16[4,272,128]{2,1,0:T(8,128)(2,1)}), bf16[4,272,128]{2,1,0:T(8,128)(2,1)S(1)}, u32[]{:S(2)}, u32[]{:S(2)}) async-start(bf16[4,272,128]{2,1,0:T(8,128)(2,1)} %get-tuple-element.27), calls=%async_computation | async-start | bytes 557056 | tf_op jit(solution)/shard_map/all_to_all | solution.py:433
  16.0 0.7 %collective-permute-start.3 = (bf16[2,256,128]{2,1,0:T(8,128)(2,1)S(1)}, bf16[2,256,128]{2,1,0:T(8,128)(2,1)S(1)}, u32[]{:S(2)}, u32[]{:S(2)}) collective-permute-start(bf16[2,256,128]{2,1,0:T(8,128)(2,1)S(1)} %get-tuple-element.25), channel_id=1, source_target_pairs={{1,4},{3,6},{4,1},{5,8},{6,3},{7,10},{8,5},{9,12},{10,7},{11,14},{... | collective-permute-start | bytes 393224 | tf_op jit(solution)/shard_map/ppermute | solution.py:362
  16.7 1.6 %collective-permute-start.2 = (bf16[8,16,128]{2,1,0:T(8,128)(2,1)S(1)}, bf16[8,16,128]{2,1,0:T(8,128)(2,1)S(1)}, u32[]{:S(2)}, u32[]{:S(2)}) collective-permute-start(bf16[8,16,128]{2,1,0:T(8,128)(2,1)S(1)} %get-tuple-element.24), channel_id=1, source_target_pairs={{0,2},{2,0},{1,3},{3,1},{4,6},{6,4},{5,7},{7,5},{8,10},{10,8},{9,1... | collective-permute-start | bytes 98312 | tf_op jit(solution)/shard_map/ppermute | solution.py:367
  18.3 0.6 %collective-permute-start.4 = (bf16[2,16,128]{2,1,0:T(8,128)(2,1)S(1)}, bf16[2,16,128]{2,1,0:T(8,128)(2,1)S(1)}, u32[]{:S(2)}, u32[]{:S(2)}) collective-permute-start(bf16[2,16,128]{2,1,0:T(8,128)(2,1)S(1)} %get-tuple-element.26), channel_id=1, source_target_pairs={{1,6},{3,4},{4,3},{5,10},{6,1},{7,8},{8,7},{9,14},{10,5},{11,12},{... | collective-permute-start | bytes 24584 | tf_op jit(solution)/shard_map/ppermute | solution.py:362
  18.9 0.0 collective-permute-done.4.mine_tail_ref
  18.9 1.8 %collective-permute-done.2.tail_ref = bf16[8,16,128]{2,1,0:T(8,128)(2,1)S(1)} collective-permute-done((bf16[8,16,128]{2,1,0:T(8,128)(2,1)S(1)}, bf16[8,16,128]{2,1,0:T(8,128)(2,1)S(1)}, u32[]{:S(2)}, u32[]{:S(2)}) %collective-permute-start.2) | collective-permute-done | bytes 32800 | tf_op jit(solution)/shard_map/ppermute | solution.py:367
  20.7 0.0 collective-permute-done.3.mine_ref
  20.7 4.9 %all-to-all-done.block_ref = bf16[4,272,128]{2,1,0:T(8,128)(2,1)S(1)} async-done(((bf16[4,272,128]{2,1,0:T(8,128)(2,1)}), bf16[4,272,128]{2,1,0:T(8,128)(2,1)S(1)}, u32[]{:S(2)}, u32[]{:S(2)}) %all-to-all-start) | async-done | bytes 278560 | tf_op jit(solution)/shard_map/all_to_all | solution.py:433
  25.6 1.7 %collective-permute-start.7 = (bf16[4,272,128]{2,1,0:T(8,128)(2,1)S(1)}, bf16[4,272,128]{2,1,0:T(8,128)(2,1)S(1)}, u32[]{:S(2)}, u32[]{:S(2)}) collective-permute-start(bf16[4,272,128]{2,1,0:T(8,128)(2,1)S(1)} %all-to-all-done.block_ref), channel_id=1, source_target_pairs={{0,1},{1,0},{2,3},{3,2},{4,5},{5,4},{6,7},{7,6},{8,9},{9,8},{10,11... | collective-permute-start | bytes 835592 | tf_op jit(solution)/shard_map/ppermute | solution.py:350
  27.3 0.1 collective-permute-start.5
  27.4 0.4 collective-permute-start.6
  27.8 0.0 copy-done.1
  27.8 0.0 copy-done
  27.8 0.3 weights.1
  28.1 0.6 %collective-permute-done.6.other_tail_ref = bf16[2,16,128]{2,1,0:T(8,128)(2,1)S(1)} collective-permute-done((bf16[2,16,128]{2,1,0:T(8,128)(2,1)S(1)}, bf16[2,16,128]{2,1,0:T(8,128)(2,1)S(1)}, u32[]{:S(2)}, u32[]{:S(2)}) %collective-permute-start.6) | collective-permute-done | bytes 8224 | tf_op jit(solution)/shard_map/ppermute | solution.py:350
  28.7 0.0 collective-permute-done.5.other_ref
  28.7 0.0 collective-permute-done.7.other_block_ref
  28.7 0.0 copy-done.8
  28.7 0.0 copy-start.6
  28.7 7.7 %forward.1 = (f32[10,272,128]{2,1,0:T(8,128)}, f32[8,256,128]{2,1,0:T(8,128)S(1)}, bf16[8,256,128]{2,1,0:T(8,128)(2,1)S(1)}, bf16[2,256,128]{2,1,0:T(8,128)(2,1)...) custom-call(bf16[8,256,128]{2,1,0:T(8,128)(2,1)S(1)} %get-tuple-element.23.x_ref, ...), custom_call_target="tpu_custom_call" | custom-call | tf_op jit(solution)/shard_map/forward/pallas_call | solution.py:42
  36.4 0.7 %collective-permute-start.9 = (bf16[2,256,128]{2,1,0:T(8,128)(2,1)S(1)}, bf16[2,256,128]{2,1,0:T(8,128)(2,1)S(1)}, u32[]{:S(2)}, u32[]{:S(2)}) collective-permute-start(bf16[2,256,128]{2,1,0:T(8,128)(2,1)S(1)} %get-tuple-element.36), channel_id=1, source_target_pairs={{1,4},{3,6},{4,1},{5,8},{6,3},{7,10},{8,5},{9,12},{10,7},{11,14},{... | collective-permute-start | bytes 393224 | tf_op jit(solution)/shard_map/ppermute | solution.py:362
  37.1 6.3 %all-to-all-start.1 = ((bf16[8,64,128]{2,1,0:T(8,128)(2,1)}), bf16[8,64,128]{2,1,0:T(8,128)(2,1)S(1)}, u32[]{:S(2)}, u32[]{:S(2)}) async-start(bf16[8,64,128]{2,1,0:T(8,128)(2,1)} %get-tuple-element.43), calls=%async_computation.1 | async-start | bytes 262144 | tf_op jit(solution)/shard_map/all_to_all | solution.py:456
  43.5 0.5 collective-permute-start.8
  44.0 0.6 %collective-permute-start.10 = (bf16[2,16,128]{2,1,0:T(8,128)(2,1)S(1)}, bf16[2,16,128]{2,1,0:T(8,128)(2,1)S(1)}, u32[]{:S(2)}, u32[]{:S(2)}) collective-permute-start(bf16[2,16,128]{2,1,0:T(8,128)(2,1)S(1)} %get-tuple-element.37), channel_id=1, source_target_pairs={{1,6},{3,4},{4,3},{5,10},{6,1},{7,8},{8,7},{9,14},{10,5},{11,12},{... | collective-permute-start | bytes 24584 | tf_op jit(solution)/shard_map/ppermute | solution.py:362
  44.6 0.0 collective-permute-done.10.mine_tail_ref
  44.7 2.7 %collective-permute-done.8.tail_ref = bf16[8,16,128]{2,1,0:T(8,128)(2,1)S(1)} collective-permute-done((bf16[8,16,128]{2,1,0:T(8,128)(2,1)S(1)}, bf16[8,16,128]{2,1,0:T(8,128)(2,1)S(1)}, u32[]{:S(2)}, u32[]{:S(2)}) %collective-permute-start.8) | collective-permute-done | bytes 32800 | tf_op jit(solution)/shard_map/ppermute | solution.py:367
  47.4 0.0 collective-permute-done.9.mine_ref
  47.4 2.9 %collective-permute-start.11 = (bf16[2,256,128]{2,1,0:T(8,128)(2,1)S(1)}, bf16[2,256,128]{2,1,0:T(8,128)(2,1)S(1)}, u32[]{:S(2)}, u32[]{:S(2)}) collective-permute-start(bf16[2,256,128]{2,1,0:T(8,128)(2,1)S(1)} %collective-permute-done.9.mine_ref), channel_id=1, source_target_pairs={{0,1},{1,0},{2,3},{3,2},{4,5},{5,4},{6,7},{7,6},{8,9},{9,8},{10,11... | collective-permute-start | bytes 393224 | tf_op jit(solution)/shard_map/ppermute | solution.py:350
  50.3 0.1 collective-permute-start.12
  50.4 0.0 all-to-all-done.1.back_ref
  50.4 0.0 copy-done.6
  50.4 1.2 %innovation.1 = bf16[4,64,128]{2,1,0:T(8,128)(2,1)} custom-call(s32[4]{0:T(128)S(1)} %copy-done.6, bf16[8,64,128]{2,1,0:T(8,128)(2,1)S(1)} %all-to-all-done.1.back_ref), custom_call_target="tpu_custom_call" | custom-call | tf_op jit(solution)/shard_map/innovation/pallas_call | solution.py:42
  51.6 0.0 collective-permute-done.12.other_tail_ref
  51.6 0.0 collective-permute-done.11.other_ref
  51.6 5.0 %backward.1 = f32[64,8,256]{2,1,0:T(8,128)} custom-call(bf16[8,256,128]{2,1,0:T(8,128)(2,1)S(1)} %get-tuple-element.34.x_ref, bf16[8,16,128]{2,1,0:T(8,128)(2,1)S(1)} %collective-permute-done.8.tail_ref, bf16[2,256,128]{2,1,0:T(8,128)(2,1)S(1)} %collective-permute-done.9.mine_ref, bf16[2,16,128]{2,1,0:T(8,128)(2,1)S(1)} %collective-permute-done.10.mine_tail_ref, ...), custom_call_target="tpu_custom_call" | custom-call | tf_op jit(solution)/shard_map/backward/pallas_call | solution.py:42
Async XLA Ops:
  0.6 27.2 %copy-start.1 = (bf16[3,3,128,128]{3,2,1,0:T(8,128)(2,1)S(1)}, bf16[3,3,128,128]{3,2,1,0:T(8,128)(2,1)}, u32[]{:S(2)}) copy-start(bf16[3,3,128,128]{3,2,1,0:T(8,128)(2,1)} %kout_ref.3) | copy-start | bytes 884740
  0.6 27.2 %copy-start = (bf16[3,3,128,128]{3,2,1,0:T(8,128)(2,1)S(1)}, bf16[3,3,128,128]{3,2,1,0:T(8,128)(2,1)}, u32[]{:S(2)}) copy-start(bf16[3,3,128,128]{3,2,1,0:T(8,128)(2,1)} %kin_ref.3) | copy-start | bytes 884740
  0.7 2.0 %collective-permute-start = (bf16[64,8,256]{2,1,0:T(8,128)(2,1)}, bf16[64,8,256]{2,1,0:T(8,128)(2,1)S(1)}, u32[]{:S(2)}, u32[]{:S(2)}) collective-permute-start(bf16[64,8,256]{2,1,0:T(8,128)(2,1)} %own_ref.1), channel_id=1, source_target_pairs={{0,1},{1,0},{2,3},{3,2},{4,5},{5,4},{6,7},{7,6},{8,9},{9,8},{10,11... | collective-permute-start | bytes 786440 | tf_op jit(solution)/shard_map/ppermute | solution.py:350
  1.2 1.5 %collective-permute-start.1 = (bf16[4,64,128]{2,1,0:T(8,128)(2,1)}, bf16[4,64,128]{2,1,0:T(8,128)(2,1)S(1)}, u32[]{:S(2)}, u32[]{:S(2)}) collective-permute-start(bf16[4,64,128]{2,1,0:T(8,128)(2,1)} %own_obs_ref.1), channel_id=1, source_target_pairs={{0,1},{1,0},{2,3},{3,2},{4,5},{5,4},{6,7},{7,6},{8,9},{9,8},{10,11... | collective-permute-start | bytes 196616 | tf_op jit(solution)/shard_map/ppermute | solution.py:350
  2.7 1.0 %copy-start.2 = (bf16[64,8,256]{2,1,0:T(8,128)(2,1)S(1)}, bf16[64,8,256]{2,1,0:T(8,128)(2,1)}, u32[]{:S(2)}) copy-start(bf16[64,8,256]{2,1,0:T(8,128)(2,1)} %own_ref.1) | copy-start | bytes 786436
  3.6 0.9 %copy-start.3 = (bf16[4,128,128]{2,1,0:T(8,128)(2,1)S(1)}, bf16[4,128,128]{2,1,0:T(8,128)(2,1)}, u32[]{:S(2)}) copy-start(bf16[4,128,128]{2,1,0:T(8,128)(2,1)} %weight_ref.1) | copy-start | bytes 393220
  4.5 0.8 %copy-start.4 = (bf16[4,64,128]{2,1,0:T(8,128)(2,1)S(1)}, bf16[4,64,128]{2,1,0:T(8,128)(2,1)}, u32[]{:S(2)}) copy-start(bf16[4,64,128]{2,1,0:T(8,128)(2,1)} %own_obs_ref.1) | copy-start | bytes 196612
  5.4 0.7 %copy-start.5 = (s32[4]{0:T(128)S(1)}, s32[4]{0:T(128)}, u32[]{:S(2)}) copy-start(s32[4]{0:T(128)} %dest_ref.3) | copy-start | bytes 52
  6.0 0.7 %copy-start.7 = (bf16[4,128]{1,0:T(4,128)(2,1)S(1)}, bf16[4,128]{1,0:T(4,128)(2,1)}, u32[]{:S(2)}) copy-start(bf16[4,128]{1,0:T(4,128)(2,1)} %precision_ref.1) | copy-start | bytes 3076
  6.7 0.7 %copy-start.9 = (s32[4]{0:T(128)S(1)}, s32[4]{0:T(128)}, u32[]{:S(2)}) copy-start(s32[4]{0:T(128)} %row_ref.1) | copy-start | bytes 52
  7.4 0.7 %copy-start.10 = (s32[4]{0:T(128)S(1)}, s32[4]{0:T(128)}, u32[]{:S(2)}) copy-start(s32[4]{0:T(128)} %col_ref.1) | copy-start | bytes 52
  8.0 20.7 %copy-start.8 = (f32[128]{0:T(128)S(1)}, f32[128]{0:T(128)}, u32[]{:S(2)}) copy-start(f32[128]{0:T(128)} %param.12) | copy-start | bytes 1540
  9.8 15.8 %all-to-all-start = ((bf16[4,272,128]{2,1,0:T(8,128)(2,1)}), bf16[4,272,128]{2,1,0:T(8,128)(2,1)S(1)}, u32[]{:S(2)}, u32[]{:S(2)}) async-start(bf16[4,272,128]{2,1,0:T(8,128)(2,1)} %get-tuple-element.27), calls=%async_computation | async-start | bytes 557056 | tf_op jit(solution)/shard_map/all_to_all | solution.py:433
  16.0 4.6 %collective-permute-start.3 = (bf16[2,256,128]{2,1,0:T(8,128)(2,1)S(1)}, bf16[2,256,128]{2,1,0:T(8,128)(2,1)S(1)}, u32[]{:S(2)}, u32[]{:S(2)}) collective-permute-start(bf16[2,256,128]{2,1,0:T(8,128)(2,1)S(1)} %get-tuple-element.25), channel_id=1, source_target_pairs={{1,4},{3,6},{4,1},{5,8},{6,3},{7,10},{8,5},{9,12},{10,7},{11,14},{... | collective-permute-start | bytes 393224 | tf_op jit(solution)/shard_map/ppermute | solution.py:362
  16.7 4.0 %collective-permute-start.2 = (bf16[8,16,128]{2,1,0:T(8,128)(2,1)S(1)}, bf16[8,16,128]{2,1,0:T(8,128)(2,1)S(1)}, u32[]{:S(2)}, u32[]{:S(2)}) collective-permute-start(bf16[8,16,128]{2,1,0:T(8,128)(2,1)S(1)} %get-tuple-element.24), channel_id=1, source_target_pairs={{0,2},{2,0},{1,3},{3,1},{4,6},{6,4},{5,7},{7,5},{8,10},{10,8},{9,1... | collective-permute-start | bytes 98312 | tf_op jit(solution)/shard_map/ppermute | solution.py:367
  18.3 0.7 %collective-permute-start.4 = (bf16[2,16,128]{2,1,0:T(8,128)(2,1)S(1)}, bf16[2,16,128]{2,1,0:T(8,128)(2,1)S(1)}, u32[]{:S(2)}, u32[]{:S(2)}) collective-permute-start(bf16[2,16,128]{2,1,0:T(8,128)(2,1)S(1)} %get-tuple-element.26), channel_id=1, source_target_pairs={{1,6},{3,4},{4,3},{5,10},{6,1},{7,8},{8,7},{9,14},{10,5},{11,12},{... | collective-permute-start | bytes 24584 | tf_op jit(solution)/shard_map/ppermute | solution.py:362
  25.6 3.1 %collective-permute-start.7 = (bf16[4,272,128]{2,1,0:T(8,128)(2,1)S(1)}, bf16[4,272,128]{2,1,0:T(8,128)(2,1)S(1)}, u32[]{:S(2)}, u32[]{:S(2)}) collective-permute-start(bf16[4,272,128]{2,1,0:T(8,128)(2,1)S(1)} %all-to-all-done.block_ref), channel_id=1, source_target_pairs={{0,1},{1,0},{2,3},{3,2},{4,5},{5,4},{6,7},{7,6},{8,9},{9,8},{10,11... | collective-permute-start | bytes 835592 | tf_op jit(solution)/shard_map/ppermute | solution.py:350
  27.3 1.4 %collective-permute-start.5 = (bf16[2,256,128]{2,1,0:T(8,128)(2,1)S(1)}, bf16[2,256,128]{2,1,0:T(8,128)(2,1)S(1)}, u32[]{:S(2)}, u32[]{:S(2)}) collective-permute-start(bf16[2,256,128]{2,1,0:T(8,128)(2,1)S(1)} %collective-permute-done.3.mine_ref), channel_id=1, source_target_pairs={{0,1},{1,0},{2,3},{3,2},{4,5},{5,4},{6,7},{7,6},{8,9},{9,8},{10,11... | collective-permute-start | bytes 393224 | tf_op jit(solution)/shard_map/ppermute | solution.py:350
  27.4 1.3 %collective-permute-start.6 = (bf16[2,16,128]{2,1,0:T(8,128)(2,1)S(1)}, bf16[2,16,128]{2,1,0:T(8,128)(2,1)S(1)}, u32[]{:S(2)}, u32[]{:S(2)}) collective-permute-start(bf16[2,16,128]{2,1,0:T(8,128)(2,1)S(1)} %collective-permute-done.4.mine_tail_ref), channel_id=1, source_target_pairs={{0,1},{1,0},{2,3},{3,2},{4,5},{5,4},{6,7},{7,6},{8,9},{9,8},{10,11... | collective-permute-start | bytes 24584 | tf_op jit(solution)/shard_map/ppermute | solution.py:350
  28.7 21.7 %copy-start.6 = (s32[4]{0:T(128)S(1)}, s32[4]{0:T(128)}, u32[]{:S(2)}) copy-start(s32[4]{0:T(128)} %dest_ref.3) | copy-start | bytes 52
  36.4 10.9 %collective-permute-start.9 = (bf16[2,256,128]{2,1,0:T(8,128)(2,1)S(1)}, bf16[2,256,128]{2,1,0:T(8,128)(2,1)S(1)}, u32[]{:S(2)}, u32[]{:S(2)}) collective-permute-start(bf16[2,256,128]{2,1,0:T(8,128)(2,1)S(1)} %get-tuple-element.36), channel_id=1, source_target_pairs={{1,4},{3,6},{4,1},{5,8},{6,3},{7,10},{8,5},{9,12},{10,7},{11,14},{... | collective-permute-start | bytes 393224 | tf_op jit(solution)/shard_map/ppermute | solution.py:362
  37.1 13.2 %all-to-all-start.1 = ((bf16[8,64,128]{2,1,0:T(8,128)(2,1)}), bf16[8,64,128]{2,1,0:T(8,128)(2,1)S(1)}, u32[]{:S(2)}, u32[]{:S(2)}) async-start(bf16[8,64,128]{2,1,0:T(8,128)(2,1)} %get-tuple-element.43), calls=%async_computation.1 | async-start | bytes 262144 | tf_op jit(solution)/shard_map/all_to_all | solution.py:456
  43.5 3.9 %collective-permute-start.8 = (bf16[8,16,128]{2,1,0:T(8,128)(2,1)S(1)}, bf16[8,16,128]{2,1,0:T(8,128)(2,1)S(1)}, u32[]{:S(2)}, u32[]{:S(2)}) collective-permute-start(bf16[8,16,128]{2,1,0:T(8,128)(2,1)S(1)} %get-tuple-element.35), channel_id=1, source_target_pairs={{0,2},{2,0},{1,3},{3,1},{4,6},{6,4},{5,7},{7,5},{8,10},{10,8},{9,1... | collective-permute-start | bytes 98312 | tf_op jit(solution)/shard_map/ppermute | solution.py:367
  44.0 0.7 %collective-permute-start.10 = (bf16[2,16,128]{2,1,0:T(8,128)(2,1)S(1)}, bf16[2,16,128]{2,1,0:T(8,128)(2,1)S(1)}, u32[]{:S(2)}, u32[]{:S(2)}) collective-permute-start(bf16[2,16,128]{2,1,0:T(8,128)(2,1)S(1)} %get-tuple-element.37), channel_id=1, source_target_pairs={{1,6},{3,4},{4,3},{5,10},{6,1},{7,8},{8,7},{9,14},{10,5},{11,12},{... | collective-permute-start | bytes 24584 | tf_op jit(solution)/shard_map/ppermute | solution.py:362
  47.4 4.2 %collective-permute-start.11 = (bf16[2,256,128]{2,1,0:T(8,128)(2,1)S(1)}, bf16[2,256,128]{2,1,0:T(8,128)(2,1)S(1)}, u32[]{:S(2)}, u32[]{:S(2)}) collective-permute-start(bf16[2,256,128]{2,1,0:T(8,128)(2,1)S(1)} %collective-permute-done.9.mine_ref), channel_id=1, source_target_pairs={{0,1},{1,0},{2,3},{3,2},{4,5},{5,4},{6,7},{7,6},{8,9},{9,8},{10,11... | collective-permute-start | bytes 393224 | tf_op jit(solution)/shard_map/ppermute | solution.py:350
  50.3 1.3 %collective-permute-start.12 = (bf16[2,16,128]{2,1,0:T(8,128)(2,1)S(1)}, bf16[2,16,128]{2,1,0:T(8,128)(2,1)S(1)}, u32[]{:S(2)}, u32[]{:S(2)}) collective-permute-start(bf16[2,16,128]{2,1,0:T(8,128)(2,1)S(1)} %collective-permute-done.10.mine_tail_ref), channel_id=1, source_target_pairs={{0,1},{1,0},{2,3},{3,2},{4,5},{5,4},{6,7},{7,6},{8,9},{9,8},{10,11... | collective-permute-start | bytes 24584 | tf_op jit(solution)/shard_map/ppermute | solution.py:350

commit v3 on v2

v3 whole, which is shorter than its diff:
```python
import jax
import jax.numpy as jnp
from jax import lax
from jax.experimental import pallas as pl
from jax.experimental.pallas import tpu as pltpu
from jax.sharding import PartitionSpec as P


PH = 4
PW = 32
CAP = 2
TAIL = 16
META = 16

keep_rate = 0.6
blend_rate = 0.4
guide_rate = 0.3

F32 = jnp.float32
BF16 = jnp.bfloat16
VMEM = pltpu.VMEM
SMEM = pltpu.SMEM
HBM = pltpu.MemorySpace.HBM
OUT = "out"


def call(kernel, outs, ins, scratch, aliases={}):
    near = lambda v, space: v if space == OUT else space(v.shape, v.dtype)
    spec = lambda space: pl.BlockSpec(memory_space=VMEM if space == OUT else space)
    run = pl.pallas_call(
        kernel,
        out_shape=[near(v, space) for v, space in outs],
        in_specs=[spec(space) for space in ins],
        out_specs=[spec(space) for _, space in outs],
        scratch_shapes=scratch,
        compiler_params=pltpu.CompilerParams(vmem_limit_bytes=24 * 1024 * 1024),
        input_output_aliases=aliases,
    )

    def apply(*args):
        return run(
            *(pltpu.with_memory_space_constraint(a, space) if space in (VMEM, HBM) else a for a, space in zip(args, ins))
        )

    return apply


def place_taps(w_ref, tap_of):
    c = w_ref.shape[0] // 4
    for b in range(3):
        for a in range(3):
            tap = tap_of(a, b)
            for row in range(2):
                at = (2 * b + row) * c
                w_ref[(a + row) * c : (a + row + 1) * c, at : at + c] = tap
        w_ref[3 * c : 4 * c, 2 * b * c : (2 * b + 1) * c] = jnp.zeros((c, c), BF16)
        w_ref[0:c, (2 * b + 1) * c : (2 * b + 2) * c] = jnp.zeros((c, c), BF16)


def weights_kernel(kin_ref, kout_ref, w1_ref, w2_ref):
    for w_ref, k_ref in ((w1_ref, kin_ref), (w2_ref, kout_ref)):
        place_taps(w_ref, lambda a, b: k_ref[a, b].astype(F32).T.astype(BF16))


def tail_of(row_ref, width):
    lane_rows = lax.broadcasted_iota(jnp.int32, (TAIL, row_ref.shape[-1]), 0)
    first = row_ref[0:TAIL, :].astype(F32)
    last = row_ref[width - TAIL : width, :].astype(F32)
    zero = jnp.zeros_like(first)
    return jnp.where(lane_rows < 2, first, jnp.where(lane_rows >= TAIL - 2, last, zero)).astype(BF16)


def write_edges(x_ref, edge_ref, tail_ref, edge_tail_ref):
    rows, width = x_ref.shape[0], x_ref.shape[1]
    first = lax.axis_index("ch") * (rows - 2)
    for h in range(rows):
        tail_ref[h] = tail_of(x_ref.at[h], width)
    for i in range(2):
        edge_ref[i] = x_ref[first + i]
        edge_tail_ref[i] = tail_ref[first + i]


def pack_kernel(
    dest_hbm,
    row_hbm,
    col_hbm,
    weight_hbm,
    obs_hbm,
    precision_hbm,
    noisy_hbm,
    chunk_ref,
    near_ref,
    dest_ref,
    row_ref,
    col_ref,
    weight_ref,
    obs_ref,
    precision_ref,
    scale_ref,
    sems,
):
    pairs = (
        (dest_hbm, dest_ref),
        (row_hbm, row_ref),
        (col_hbm, col_ref),
        (weight_hbm, weight_ref),
        (obs_hbm, obs_ref),
        (precision_hbm, precision_ref),
        (noisy_hbm, near_ref),
    )
    copies = [pltpu.make_async_copy(source, target, sems.at[n]) for n, (source, target) in enumerate(pairs)]
    for copy in copies:
        copy.start()
    core = lax.axis_index("ch")
    blocks, obs, _ = weight_ref.shape
    half = obs_ref.shape[1]
    first_meta = obs + CAP * half

    def clear(slot, _):
        chunk_ref[slot] = jnp.zeros(chunk_ref.shape[1:], BF16)
        return 0

    lax.fori_loop(0, chunk_ref.shape[0], clear, 0)
    for copy in copies[:-1]:
        copy.wait()
    scale_ref[...] = precision_ref[...].astype(F32)
    meta_rows = lax.broadcasted_iota(jnp.int32, (META, obs), 0)

    def pack(b, _):
        dest = dest_ref[b]
        rank = lax.fori_loop(0, b, lambda j, n: n + (dest_ref[j] == dest).astype(jnp.int32), 0)
        chunk_ref[dest, pl.ds(pl.multiple_of(obs + rank * half, 16), half), :] = obs_ref[b]

        @pl.when(rank == core)
        def _():
            chunk_ref[dest, 0:obs, :] = weight_ref[b]
            row = row_ref[b].astype(F32)
            high = lax.div(col_ref[b], 16).astype(F32)
            low = lax.rem(col_ref[b], 16).astype(F32)
            meta = jnp.where(
                meta_rows == 0,
                jnp.broadcast_to(scale_ref[pl.ds(b, 1), :], (META, obs)),
                jnp.where(meta_rows == 1, row, jnp.where(meta_rows == 2, high, low)),
            )
            chunk_ref[dest, first_meta : first_meta + META, :] = meta.astype(BF16)

        return 0

    lax.fori_loop(0, blocks, pack, 0)
    copies[-1].wait()


def prep_kernel(own_ref, other_ref, x_ref, edge_ref, tail_ref, edge_tail_ref, flat_ref):
    core = lax.axis_index("ch")
    half, rows, width = own_ref.shape

    def place(ref, first):
        for part in range(width // 128):
            piece = ref[:, :, part * 128 : (part + 1) * 128].astype(F32)
            flat_ref[part, pl.ds(pl.multiple_of(first * rows, 8), half * rows), :] = piece.reshape(half * rows, 128)

    place(own_ref, core * half)
    place(other_ref, (1 - core) * half)
    for h in range(rows):
        for part in range(width // 128):
            plane = flat_ref[part, pl.ds(h, 2 * half, stride=rows), :]
            x_ref[h, part * 128 : (part + 1) * 128, :] = plane.T.astype(BF16)
    write_edges(x_ref, edge_ref, tail_ref, edge_tail_ref)


def fill_extended(ext_ref, x_ref, tail_ref, mine_ref, mine_tail_ref, other_ref, other_tail_ref):
    rows, width = x_ref.shape[0], x_ref.shape[1]
    core = lax.axis_index("ch")
    for i in range(2):
        mine = core * (rows + 2) + i
        other = (1 - core) * (rows + 2) + i
        ext_ref[mine, 0:width, :] = mine_ref[i]
        ext_ref[mine, width : width + TAIL, :] = mine_tail_ref[i]
        ext_ref[other, 0:width, :] = other_ref[i]
        ext_ref[other, width : width + TAIL, :] = other_tail_ref[i]
    for h in range(rows):
        ext_ref[h + 2, 0:width, :] = x_ref[h]
        ext_ref[h + 2, width : width + TAIL, :] = tail_ref[h]


def row_pair(src_ref, w_ref, first):
    c = src_ref.shape[-1]
    wide = src_ref.shape[1]
    lhs = jnp.concatenate([src_ref[first + k] for k in range(4)], axis=1)
    y = jnp.dot(lhs, w_ref[...], preferred_element_type=F32)
    out = []
    for row in range(2):
        left, mid, right = (y[:, (2 * b + row) * c : (2 * b + row + 1) * c] for b in range(3))
        out.append(pltpu.roll(left, 1, 0) + mid + pltpu.roll(right, wide - 1, 0))
    return out


def inside(ext_row, ext_rows):
    at = lax.axis_index("lat")
    last = lax.axis_size("lat") - 1
    return ((ext_row > 0) | (at > 0)) & ((ext_row < ext_rows - 1) | (at < last))


def own_pair(first, second):
    core = lax.axis_index("ch")
    half = first.shape[-1] // 2
    lane = lax.broadcasted_iota(jnp.int32, first.shape, len(first.shape) - 1)
    stays = jnp.where(core == 0, first, second)
    moves = pltpu.roll(jnp.where(core == 0, second, first), half, len(first.shape) - 1)
    low = (lane < half).astype(jnp.int32)
    return jnp.where(low == 1 - core, stays, moves)


def forward_kernel(
    x_ref,
    tail_ref,
    mine_ref,
    mine_tail_ref,
    other_ref,
    other_tail_ref,
    w1_ref,
    w2_ref,
    bias_ref,
    block_ref,
    other_block_ref,
    slope_ref,
    base_ref,
    g_ref,
    edge_ref,
    gtail_ref,
    edge_tail_ref,
    inn_ref,
    ext_ref,
    hidden_ref,
    den_ref,
    field_ref,
    turned_ref,
    value_ref,
    scale_ref,
    code_ref,
):
    core = lax.axis_index("ch")
    rows, width, c = x_ref.shape
    half = inn_ref.shape[1]
    sources, obs = block_ref.shape[0], block_ref.shape[2]
    fill_extended(ext_ref, x_ref, tail_ref, mine_ref, mine_tail_ref, other_ref, other_tail_ref)

    def read(source, cap, first, count):
        at = slice(first, first + count)
        return jnp.where(core == cap, block_ref[source, at, :], other_block_ref[source, at, :])

    def locate(source, cap):
        meta = read(source, cap, obs + c, META).astype(F32)
        code = meta[1:2, :] * 65536.0 + meta[2:3, :] * 16.0 + meta[3:4, :]
        code_ref[source * CAP + cap] = jnp.max(code).astype(jnp.int32)

    def turn(source, cap):
        slot = source * CAP + cap
        turned_ref[slot] = read(source, cap, 0, obs).T
        at = slice(obs + cap * half, obs + (cap + 1) * half)
        mine, theirs = block_ref[source, at, :], other_block_ref[source, at, :]
        low, high = jnp.where(core == 0, mine, theirs), jnp.where(core == 0, theirs, mine)
        value_ref[slot] = jnp.concatenate([low, high], axis=0).T
        row = read(source, cap, obs + c, META).astype(F32)[0:1, :]
        scale_ref[slot] = jnp.broadcast_to(row, (c, obs)).T

    def each(task, first, last):
        if last - first <= 8:
            for source in range(first, last):
                for cap in range(CAP):
                    task(source, cap)
            return

        def step(source, _):
            for cap in range(CAP):
                task(source, cap)
            return 0

        lax.fori_loop(first, last, step, 0)

    each(locate, 0, sources)
    bias = bias_ref[...]
    for g in range((rows + 2) // 2):
        for i, y in enumerate(row_pair(ext_ref, w1_ref, 2 * g)):
            r = 2 * g + i
            pre = y + bias
            s = 1.0 / (1.0 + jnp.exp(-pre))
            slope_ref[r] = s * (1.0 + pre * (1.0 - s))
            hidden_ref[r] = jnp.where(inside(r, rows + 2), pre * s, 0.0).astype(BF16)
    groups = rows // 2
    for g in range(groups):
        each(turn, sources * g // groups, sources * (g + 1) // groups)
        for i, y in enumerate(row_pair(hidden_ref, w2_ref, 2 * g)):
            r = 2 * g + i
            noisy = x_ref[r].astype(F32)
            den_ref[r] = (noisy + y[0:width, :]).astype(BF16).astype(F32)
            field_ref[r] = jnp.zeros((width, c), F32)

    def observe(source, cap):
        slot = source * CAP + cap
        code = code_ref[slot]
        row = lax.shift_right_logical(code, 16)
        col = lax.bitwise_and(code, 65535)
        patch = jnp.concatenate([den_ref[row + i, pl.ds(col, PW), :] for i in range(PH)], axis=0).astype(BF16)
        predicted = jnp.dot(read(source, cap, 0, obs), patch, preferred_element_type=F32)
        residual = predicted - value_ref[slot].astype(F32)
        weighted = (residual * scale_ref[slot]).astype(BF16)
        pulled = jnp.dot(turned_ref[slot], weighted, preferred_element_type=F32)
        for i in range(PH):
            field_ref[row + i, pl.ds(col, PW), :] += pulled[i * PW : (i + 1) * PW, :]
        turned = residual.astype(BF16).T
        inn_ref[slot] = jnp.where(core == 0, turned[0:half], turned[half : 2 * half])

    each(observe, 0, sources)

    for g in range(groups):
        base = []
        for r in (2 * g, 2 * g + 1):
            field = field_ref[r]
            noisy = ext_ref[r + 2, 0:width, :].astype(F32)
            base.append(keep_rate * noisy + blend_rate * den_ref[r] - guide_rate * field)
            g_ref[r] = field.astype(BF16)
        base_ref[g] = own_pair(*base)
    write_edges(g_ref, edge_ref, gtail_ref, edge_tail_ref)


def backward_kernel(
    x_ref,
    tail_ref,
    mine_ref,
    mine_tail_ref,
    other_ref,
    other_tail_ref,
    kin_ref,
    kout_ref,
    base_ref,
    slope_ref,
    next_ref,
    ext_ref,
    grad_ref,
    flat_ref,
    w3_ref,
    w4_ref,
):
    rows, width, c = x_ref.shape
    wide = ext_ref.shape[1]
    half = next_ref.shape[0]
    fill_extended(ext_ref, x_ref, tail_ref, mine_ref, mine_tail_ref, other_ref, other_tail_ref)
    place_taps(w3_ref, lambda a, b: kout_ref[2 - a, 2 - b])
    zero = jnp.zeros((c, c), F32)
    for b in range(3):
        taps = [zero] + [kin_ref[2 - a, 2 - b].astype(F32) for a in range(3)] + [zero]
        for k in range(4):
            w4_ref[k * c : (k + 1) * c, b * c : (b + 1) * c] = own_pair(taps[k + 1], taps[k]).astype(BF16)

    for g in range((rows + 2) // 2):
        for i, y in enumerate(row_pair(ext_ref, w3_ref, 2 * g)):
            r = 2 * g + i
            grad_ref[r] = jnp.where(inside(r, rows + 2), y * slope_ref[r], 0.0).astype(BF16)

    for g in range(rows // 2):
        lhs = jnp.concatenate([grad_ref[2 * g + k] for k in range(4)], axis=1)
        y = jnp.dot(lhs, w4_ref[...], preferred_element_type=F32)
        y = pltpu.roll(y[:, 0:c], 1, 0) + y[:, c : 2 * c] + pltpu.roll(y[:, 2 * c : 3 * c], wide - 1, 0)
        out = base_ref[g] - guide_rate * y[0:width, :]
        for part in range(width // 128):
            plane = out[part * 128 : (part + 1) * 128, :].T
            for i in range(2):
                flat_ref[part, pl.ds(2 * g + i, half, stride=rows), :] = plane[i * half : (i + 1) * half]
    for part in range(width // 128):
        next_ref[:, :, part * 128 : (part + 1) * 128] = flat_ref[part].reshape(half, rows, 128)


def return_kernel(dest_ref, back_ref, inn_ref):
    def take(b, _):
        dest = dest_ref[b]
        rank = lax.fori_loop(0, b, lambda j, n: n + (dest_ref[j] == dest).astype(jnp.int32), 0)
        inn_ref[b] = back_ref[dest * CAP + rank]
        return 0

    lax.fori_loop(0, inn_ref.shape[0], take, 0)


def swapped(value):
    return lax.ppermute(value, "ch", [(0, 1), (1, 0)])


def from_row_neighbour(value, lon_step):
    lats, lons = lax.axis_size("lat"), lax.axis_size("lon")
    pairs = []
    for i in range(lats):
        for j in range(lons):
            for core, step in ((0, -1), (1, 1)):
                if 0 <= i + step < lats:
                    to = (i + step) * lons + (j + lon_step) % lons
                    pairs.append(((i * lons + j) * 2 + core, to * 2 + 1 - core))
    return lax.ppermute(value, ("lat", "lon", "ch"), pairs)


def from_lon_neighbour(value, lon_step):
    lons = lax.axis_size("lon")
    return lax.ppermute(value, "lon", [(j, (j + lon_step) % lons) for j in range(lons)])


def both_sides(move, value):
    if lax.axis_size("lon") == 2:
        return move(value, 1)
    from_right = move(value, -1)
    from_left = move(value, 1)
    at = lax.broadcasted_iota(jnp.int32, (1, TAIL, 1), 1)
    return jnp.where(at < TAIL // 2, from_right, from_left)


def exchanged(edge, tail, edge_tail, along):
    mine_tail = both_sides(from_row_neighbour, edge_tail)
    mine = from_row_neighbour(edge, 0)
    beside = both_sides(from_lon_neighbour, tail)
    *halo, along = lax.optimization_barrier((beside, mine, mine_tail, along))
    halo = tuple(halo) + (swapped(halo[1]), swapped(halo[2]))
    return halo, along


def shape(dims, dtype):
    return jax.ShapeDtypeStruct(dims, dtype)


def edge_shapes(rows, width, c):
    return [
        (shape((2, width, c), BF16), VMEM),
        (shape((rows, TAIL, c), BF16), VMEM),
        (shape((2, TAIL, c), BF16), VMEM),
    ]


def body(
    noisy_state,
    kernel_in,
    bias_in,
    kernel_out,
    interp_weight,
    observed,
    obs_precision,
    dest_tile,
    row_offset,
    col_offset,
):
    half, rows, width = noisy_state.shape
    c = kernel_in.shape[-1]
    blocks, obs, _ = interp_weight.shape
    lats = lax.axis_size("lat")
    slots = lats * CAP
    wide = width + TAIL
    other = swapped(noisy_state)
    chunk_shape = shape((lats, obs + CAP * half + META, obs), BF16)
    chunk, near = call(
        pack_kernel,
        [(chunk_shape, VMEM), (shape(noisy_state.shape, BF16), VMEM)],
        [HBM] * 7,
        [
            SMEM((blocks,), jnp.int32),
            SMEM((blocks,), jnp.int32),
            SMEM((blocks,), jnp.int32),
            VMEM(interp_weight.shape, BF16),
            VMEM(observed.shape, BF16),
            VMEM(obs_precision.shape, BF16),
            VMEM(obs_precision.shape, F32),
            pltpu.SemaphoreType.DMA((7,)),
        ],
    )(dest_tile, row_offset, col_offset, interp_weight, observed, obs_precision, noisy_state)
    block = lax.all_to_all(chunk, "lat", split_axis=0, concat_axis=0, tiled=True)
    x, *edges = call(
        prep_kernel,
        [(shape((rows, width, c), BF16), VMEM), *edge_shapes(rows, width, c)],
        [VMEM] * 2,
        [VMEM((width // 128, c * rows, 128), F32)],
    )(near, other)
    w1, w2 = call(weights_kernel, [(shape((4 * c, 6 * c), BF16), VMEM)] * 2, [VMEM] * 2, [])(kernel_in, kernel_out)
    halo, block = exchanged(*edges, block)
    slope, base, g, *edges, inn = call(
        forward_kernel,
        [
            (shape((rows + 2, wide, c), F32), VMEM),
            (shape((rows // 2, width, c), F32), VMEM),
            (shape((rows, width, c), BF16), VMEM),
            *edge_shapes(rows, width, c),
            (shape((slots, half, obs), BF16), VMEM),
        ],
        [VMEM] * 11,
        [
            VMEM((rows + 4, wide, c), BF16),
            VMEM((rows + 2, wide, c), BF16),
            VMEM((rows, width, c), F32),
            VMEM((rows, width, c), F32),
            VMEM((slots, obs, obs), BF16),
            VMEM((slots, obs, c), BF16),
            VMEM((slots, obs, c), F32),
            SMEM((slots,), jnp.int32),
        ],
        {0: 2, 2: 3, 1: 4, 3: 5},
    )(x, *halo, w1, w2, bias_in.reshape(1, c), block, swapped(block))
    halo, _ = exchanged(*edges, ())
    back = lax.all_to_all(inn, "lat", split_axis=0, concat_axis=0, tiled=True)
    (next_state,) = call(
        backward_kernel,
        [(shape((half, rows, width), F32), OUT)],
        [VMEM] * 10,
        [
            VMEM((rows + 4, wide, c), BF16),
            VMEM((rows + 2, wide, c), BF16),
            VMEM((width // 128, half * rows, 128), F32),
            VMEM((4 * c, 6 * c), BF16),
            VMEM((4 * c, 3 * c), BF16),
        ],
    )(g, *halo, kernel_in, kernel_out, base, slope)
    (innovation,) = call(return_kernel, [(shape(observed.shape, BF16), OUT)], [SMEM, VMEM], [])(dest_tile, back)
    return next_state, innovation


def solution(mesh):
    return jax.shard_map(
        body,
        mesh=mesh,
        in_specs=(
            P(("grp", "ch"), "lat", "lon"),
            P(),
            P(),
            P(),
            P(("grp", "lat", "lon"), None, None),
            P(("grp", "lat", "lon"), "ch", None),
            P(("grp", "lat", "lon"), None),
            P(("grp", "lat", "lon")),
            P(("grp", "lat", "lon")),
            P(("grp", "lat", "lon")),
        ),
        out_specs=(P(("grp", "ch"), "lat", "lon"), P(("grp", "lat", "lon"), "ch", None)),
        check_vma=False,
    )
```

time: 57.2 us -> 47.5 us (0.83)
  Pallas kernels: 16.1 us -> 11.4 us
  local copies, waits for them, and re-layouts: 5.35 us -> 0.67 us
  waiting for transfers between devices: 11.4 us -> 9.43 us
  starting transfers between devices: 23.1 us -> 24.9 us
    unnamed x22 -> x10, local copies, waits for them, and re-layouts: 5.35 us -> 0.67 us
    pallas_call x5 -> x6, Pallas kernels: 16.1 us -> 11.4 us  [apply(): run(*(pltpu.with_memory_space_constraint(a, space) if space in (VMEM, HBM...]
    all_to_all x1, waiting for transfers between devices: 4.91 us -> 2.61 us  [body(): lax.all_to_all(chunk, 'lat', split_axis=0, concat_axis=0, tiled=True)]
    ppermute x7 -> x6, starting transfers between devices: 5.83 us -> 7.5 us  [swapped(): return lax.ppermute(value, 'ch', [(0, 1), (1, 0)])]
    ppermute x7 -> x6, waiting for transfers between devices: 1.99 us -> 2.34 us  [swapped(): return lax.ppermute(value, 'ch', [(0, 1), (1, 0)])]
  transfers between devices with their start and end apart: 15 -> 14, of which waited for: 5 -> 5; matrix products, arithmetic and copies ran while one was open for 0% -> 0% of each run, Pallas kernels for 3% -> 4%
where the time goes in v3:
time: 47.5 us; the launch traced here: 47.1 us
  starting transfers between devices  24.9 us (52%)
  Pallas kernels  11.4 us (24%)
  waiting for transfers between devices  9.43 us (20%)
  between operations  0.76 us (2%)
  local copies, waits for them, and re-layouts  0.67 us (1%)
    pallas_call x6, Pallas kernels, apply(): run(*(pltpu.with_memory_space_constraint(a, space) if space in (VMEM, HBM...  11.4 us
    ppermute x6, starting transfers between devices, swapped(): return lax.ppermute(value, 'ch', [(0, 1), (1, 0)])  7.5 us
    all_to_all x1, starting transfers between devices, body(): lax.all_to_all(chunk, 'lat', split_axis=0, concat_axis=0, tiled=True)  6.36 us
    all_to_all x1, starting transfers between devices, body(): back = lax.all_to_all(inn, 'lat', split_axis=0, concat_axis=0, tiled=True)  6.32 us
    ppermute x2, waiting for transfers between devices, from_lon_neighbour(): lax.ppermute(value, 'lon', [(j, (j + lon_step) % lons) for j in range(lon...  4.47 us
    ppermute x4, starting transfers between devices, from_row_neighbour(): return lax.ppermute(value, ('lat', 'lon', 'ch'), pairs)  2.62 us
    all_to_all x1, waiting for transfers between devices, body(): lax.all_to_all(chunk, 'lat', split_axis=0, concat_axis=0, tiled=True)  2.61 us
    ppermute x6, waiting for transfers between devices, swapped(): return lax.ppermute(value, 'ch', [(0, 1), (1, 0)])  2.34 us
  transfers between devices with their start and end apart: 14, of which 5 were waited for; matrix products, arithmetic and copies ran while one was open for 0% of the time, Pallas kernels for 4%

profile of v3, /device:TPU:0, one launch (start us, length us, event | category | flops | bytes accessed | tf_op | source)
XLA Modules:
  0.0 47.1 jit_solution(7626802790903190068)
XLA Ops:
  0.6 0.0 copy-start.1
  0.6 0.0 copy-start
  0.7 0.0 copy-start.4
  0.7 1.9 %shard_map.113 = (bf16[4,272,128]{2,1,0:T(8,128)(2,1)}, bf16[64,8,256]{2,1,0:T(8,128)(2,1)S(1)}) custom-call(s32[4]{0:T(128)} %dest_ref.1, s32[4]{0:T(128)} %row_hbm.1, s32[4]{0:T(128)} %col_hbm.1, bf16[4,128,128]{2,1,0:T(8,128)(2,1)} %weight_hbm.1, bf16[4,64,128]{2,1,0:T(8,128)(2,1)} %obs_hbm.1, bf16[4,128]{1,0:T(4,128)(2,1)} %precision_hbm.1, ...), custom_call_target="tpu_custom_call" | custom-call | tf_op jit(solution)/shard_map/pallas_call | solution.py:41
  2.6 6.4 %all-to-all-start = ((bf16[4,272,128]{2,1,0:T(8,128)(2,1)}), bf16[4,272,128]{2,1,0:T(8,128)(2,1)S(1)}, u32[]{:S(2)}, u32[]{:S(2)}) async-start(bf16[4,272,128]{2,1,0:T(8,128)(2,1)} %get-tuple-element.29), calls=%async_computation | async-start | bytes 557056 | tf_op jit(solution)/shard_map/all_to_all | solution.py:470
  8.9 0.0 collective-permute-start
  8.9 1.7 %collective-permute-done.other_ref = bf16[64,8,256]{2,1,0:T(8,128)(2,1)S(1)} collective-permute-done((bf16[64,8,256]{2,1,0:T(8,128)(2,1)}, bf16[64,8,256]{2,1,0:T(8,128)(2,1)S(1)}, u32[]{:S(2)}, u32[]{:S(2)}) %collective-permute-start) | collective-permute-done | bytes 262176 | tf_op jit(solution)/shard_map/ppermute | solution.py:385
  10.7 0.4 shard_map.114
  11.0 0.7 %collective-permute-start.2 = (bf16[2,256,128]{2,1,0:T(8,128)(2,1)S(1)}, bf16[2,256,128]{2,1,0:T(8,128)(2,1)S(1)}, u32[]{:S(2)}, u32[]{:S(2)}) collective-permute-start(bf16[2,256,128]{2,1,0:T(8,128)(2,1)S(1)} %get-tuple-element.27), channel_id=1, source_target_pairs={{1,4},{3,6},{4,1},{5,8},{6,3},{7,10},{8,5},{9,12},{10,7},{11,14},{... | collective-permute-start | bytes 393224 | tf_op jit(solution)/shard_map/ppermute | solution.py:397
  11.7 1.6 %collective-permute-start.1 = (bf16[8,16,128]{2,1,0:T(8,128)(2,1)S(1)}, bf16[8,16,128]{2,1,0:T(8,128)(2,1)S(1)}, u32[]{:S(2)}, u32[]{:S(2)}) collective-permute-start(bf16[8,16,128]{2,1,0:T(8,128)(2,1)S(1)} %get-tuple-element.26), channel_id=1, source_target_pairs={{0,2},{2,0},{1,3},{3,1},{4,6},{6,4},{5,7},{7,5},{8,10},{10,8},{9,1... | collective-permute-start | bytes 98312 | tf_op jit(solution)/shard_map/ppermute | solution.py:402
  13.2 0.6 %collective-permute-start.3 = (bf16[2,16,128]{2,1,0:T(8,128)(2,1)S(1)}, bf16[2,16,128]{2,1,0:T(8,128)(2,1)S(1)}, u32[]{:S(2)}, u32[]{:S(2)}) collective-permute-start(bf16[2,16,128]{2,1,0:T(8,128)(2,1)S(1)} %get-tuple-element.28), channel_id=1, source_target_pairs={{1,6},{3,4},{4,3},{5,10},{6,1},{7,8},{8,7},{9,14},{10,5},{11,12},{... | collective-permute-start | bytes 24584 | tf_op jit(solution)/shard_map/ppermute | solution.py:397
  13.9 0.0 collective-permute-done.3.mine_tail_ref
  13.9 1.8 %collective-permute-done.1.tail_ref = bf16[8,16,128]{2,1,0:T(8,128)(2,1)S(1)} collective-permute-done((bf16[8,16,128]{2,1,0:T(8,128)(2,1)S(1)}, bf16[8,16,128]{2,1,0:T(8,128)(2,1)S(1)}, u32[]{:S(2)}, u32[]{:S(2)}) %collective-permute-start.1) | collective-permute-done | bytes 32800 | tf_op jit(solution)/shard_map/ppermute | solution.py:402
  15.7 0.0 collective-permute-done.2.mine_ref
  15.7 2.6 %all-to-all-done.block_ref = bf16[4,272,128]{2,1,0:T(8,128)(2,1)S(1)} async-done(((bf16[4,272,128]{2,1,0:T(8,128)(2,1)}), bf16[4,272,128]{2,1,0:T(8,128)(2,1)S(1)}, u32[]{:S(2)}, u32[]{:S(2)}) %all-to-all-start) | async-done | bytes 278560 | tf_op jit(solution)/shard_map/all_to_all | solution.py:470
  18.3 4.0 %collective-permute-start.6 = (bf16[4,272,128]{2,1,0:T(8,128)(2,1)S(1)}, bf16[4,272,128]{2,1,0:T(8,128)(2,1)S(1)}, u32[]{:S(2)}, u32[]{:S(2)}) collective-permute-start(bf16[4,272,128]{2,1,0:T(8,128)(2,1)S(1)} %all-to-all-done.block_ref), channel_id=1, source_target_pairs={{0,1},{1,0},{2,3},{3,2},{4,5},{5,4},{6,7},{7,6},{8,9},{9,8},{10,11... | collective-permute-start | bytes 835592 | tf_op jit(solution)/shard_map/ppermute | solution.py:385
  22.3 0.1 collective-permute-start.4
  22.4 0.4 collective-permute-start.5
  22.8 0.0 copy-done.1
  22.8 0.0 copy-done
  22.8 0.3 shard_map.115
  23.1 0.6 %collective-permute-done.5.other_tail_ref = bf16[2,16,128]{2,1,0:T(8,128)(2,1)S(1)} collective-permute-done((bf16[2,16,128]{2,1,0:T(8,128)(2,1)S(1)}, bf16[2,16,128]{2,1,0:T(8,128)(2,1)S(1)}, u32[]{:S(2)}, u32[]{:S(2)}) %collective-permute-start.5) | collective-permute-done | bytes 8224 | tf_op jit(solution)/shard_map/ppermute | solution.py:385
  23.7 0.0 collective-permute-done.4.other_ref
  23.7 0.0 collective-permute-done.6.other_block_ref
  23.7 0.0 copy-done.4
  23.7 0.0 copy-start.3
  23.7 3.8 %shard_map.116 = (f32[10,272,128]{2,1,0:T(8,128)S(1)}, f32[4,256,128]{2,1,0:T(8,128)S(1)}, bf16[8,256,128]{2,1,0:T(8,128)(2,1)S(1)}, bf16[2,256,128]{2,1,0:T(8,1...) custom-call(bf16[8,256,128]{2,1,0:T(8,128)(2,1)S(1)} %get-tuple-elem, ...), custom_call_target="tpu_custom_call", output_to_operand_aliasing={{2}: (0, {}), {3}: (2, {}), {4}: (1, {}), {5}: (3, {})} | custom-call | tf_op jit(solution)/shard_map/pallas_call | solution.py:41
  27.5 0.0 copy-start.2
  27.5 0.6 %copy-done.2 = bf16[8,64,128]{2,1,0:T(8,128)(2,1)} copy-done((bf16[8,64,128]{2,1,0:T(8,128)(2,1)}, bf16[8,64,128]{2,1,0:T(8,128)(2,1)S(1)}, u32[]{:S(2)}) %copy-start.2) | copy-done | bytes 131096
  28.1 0.7 %collective-permute-start.8 = (bf16[2,256,128]{2,1,0:T(8,128)(2,1)S(1)}, bf16[2,256,128]{2,1,0:T(8,128)(2,1)S(1)}, u32[]{:S(2)}, u32[]{:S(2)}) collective-permute-start(bf16[2,256,128]{2,1,0:T(8,128)(2,1)S(1)} %get-tuple-element.38), channel_id=1, source_target_pairs={{1,4},{3,6},{4,1},{5,8},{6,3},{7,10},{8,5},{9,12},{10,7},{11,14},{... | collective-permute-start | bytes 393224 | tf_op jit(solution)/shard_map/ppermute | solution.py:397
  28.8 6.3 %all-to-all-start.1 = ((bf16[8,64,128]{2,1,0:T(8,128)(2,1)}), bf16[8,64,128]{2,1,0:T(8,128)(2,1)S(1)}, u32[]{:S(2)}, u32[]{:S(2)}) async-start(bf16[8,64,128]{2,1,0:T(8,128)(2,1)} %copy-done.2), calls=%async_computation.1 | async-start | bytes 262144 | tf_op jit(solution)/shard_map/all_to_all | solution.py:502
  35.1 0.5 %collective-permute-start.7 = (bf16[8,16,128]{2,1,0:T(8,128)(2,1)S(1)}, bf16[8,16,128]{2,1,0:T(8,128)(2,1)S(1)}, u32[]{:S(2)}, u32[]{:S(2)}) collective-permute-start(bf16[8,16,128]{2,1,0:T(8,128)(2,1)S(1)} %get-tuple-element.37), channel_id=1, source_target_pairs={{0,2},{2,0},{1,3},{3,1},{4,6},{6,4},{5,7},{7,5},{8,10},{10,8},{9,1... | collective-permute-start | bytes 98312 | tf_op jit(solution)/shard_map/ppermute | solution.py:402
  35.7 0.6 %collective-permute-start.9 = (bf16[2,16,128]{2,1,0:T(8,128)(2,1)S(1)}, bf16[2,16,128]{2,1,0:T(8,128)(2,1)S(1)}, u32[]{:S(2)}, u32[]{:S(2)}) collective-permute-start(bf16[2,16,128]{2,1,0:T(8,128)(2,1)S(1)} %get-tuple-element.39), channel_id=1, source_target_pairs={{1,6},{3,4},{4,3},{5,10},{6,1},{7,8},{8,7},{9,14},{10,5},{11,12},{... | collective-permute-start | bytes 24584 | tf_op jit(solution)/shard_map/ppermute | solution.py:397
  36.3 0.0 collective-permute-done.9.mine_tail_ref
  36.3 2.7 %collective-permute-done.7.tail_ref = bf16[8,16,128]{2,1,0:T(8,128)(2,1)S(1)} collective-permute-done((bf16[8,16,128]{2,1,0:T(8,128)(2,1)S(1)}, bf16[8,16,128]{2,1,0:T(8,128)(2,1)S(1)}, u32[]{:S(2)}, u32[]{:S(2)}) %collective-permute-start.7) | collective-permute-done | bytes 32800 | tf_op jit(solution)/shard_map/ppermute | solution.py:402
  39.0 0.0 collective-permute-done.8.mine_ref
  39.0 2.9 %collective-permute-start.10 = (bf16[2,256,128]{2,1,0:T(8,128)(2,1)S(1)}, bf16[2,256,128]{2,1,0:T(8,128)(2,1)}, u32[]{:S(2)}, u32[]{:S(2)}) collective-permute-start(bf16[2,256,128]{2,1,0:T(8,128)(2,1)S(1)} %collective-permute-done.8.mine_ref), channel_id=1, source_target_pairs={{0,1},{1,0},{2,3},{3,2},{4,5},{5,4},{6,7},{7,6},{8,9},{9,8},{10,11... | collective-permute-start | bytes 393224 | tf_op jit(solution)/shard_map/ppermute | solution.py:385
  42.0 0.1 collective-permute-start.11
  42.0 0.0 all-to-all-done.1.back_ref
  42.0 0.0 copy-done.3
  42.0 1.2 %shard_map.118 = bf16[4,64,128]{2,1,0:T(8,128)(2,1)} custom-call(s32[4]{0:T(128)S(1)} %copy-done.3, bf16[8,64,128]{2,1,0:T(8,128)(2,1)S(1)} %all-to-all-done.1.back_ref), custom_call_target="tpu_custom_call" | custom-call | tf_op jit(solution)/shard_map/pallas_call | solution.py:41
  43.3 0.0 collective-permute-done.11.other_tail_ref
  43.3 0.0 collective-permute-done.10.other_ref
  43.3 3.9 %shard_map.117 = f32[64,8,256]{2,1,0:T(8,128)} custom-call(bf16[8,256,128]{2,1,0:T(8,128)(2,1)S(1)} %get-tuple-element.36.x_ref, bf16[8,16,128]{2,1,0:T(8,128)(2,1)S(1)} %collective-permute-done.7.tail_ref, bf16[2,256,128]{2,1,0:T(8,128)(2,1)S(1)} %collective-permute-done.8.mine_ref, bf16[2,16,128]{2,1,0:T(8,128)(2,1)S(1)} %collective-permute-done.9.mine_tail_ref, ...), custom_call_target="tpu_custom_call" | custom-call | tf_op jit(solution)/shard_map/pallas_call | solution.py:41
Async XLA Ops:
  0.6 22.2 %copy-start.1 = (bf16[3,3,128,128]{3,2,1,0:T(8,128)(2,1)S(1)}, bf16[3,3,128,128]{3,2,1,0:T(8,128)(2,1)}, u32[]{:S(2)}) copy-start(bf16[3,3,128,128]{3,2,1,0:T(8,128)(2,1)} %kout_ref.3) | copy-start | bytes 884740
  0.6 22.2 %copy-start = (bf16[3,3,128,128]{3,2,1,0:T(8,128)(2,1)S(1)}, bf16[3,3,128,128]{3,2,1,0:T(8,128)(2,1)}, u32[]{:S(2)}) copy-start(bf16[3,3,128,128]{3,2,1,0:T(8,128)(2,1)} %kin_ref.3) | copy-start | bytes 884740
  0.7 23.0 %copy-start.4 = (f32[128]{0:T(128)S(1)}, f32[128]{0:T(128)}, u32[]{:S(2)}) copy-start(f32[128]{0:T(128)} %param.12) | copy-start | bytes 1540
  2.6 15.7 %all-to-all-start = ((bf16[4,272,128]{2,1,0:T(8,128)(2,1)}), bf16[4,272,128]{2,1,0:T(8,128)(2,1)S(1)}, u32[]{:S(2)}, u32[]{:S(2)}) async-start(bf16[4,272,128]{2,1,0:T(8,128)(2,1)} %get-tuple-element.29), calls=%async_computation | async-start | bytes 557056 | tf_op jit(solution)/shard_map/all_to_all | solution.py:470
  8.9 1.7 %collective-permute-start = (bf16[64,8,256]{2,1,0:T(8,128)(2,1)}, bf16[64,8,256]{2,1,0:T(8,128)(2,1)S(1)}, u32[]{:S(2)}, u32[]{:S(2)}) collective-permute-start(bf16[64,8,256]{2,1,0:T(8,128)(2,1)} %noisy_hbm.1), channel_id=1, source_target_pairs={{0,1},{1,0},{2,3},{3,2},{4,5},{5,4},{6,7},{7,6},{8,9},{9,8},{10,11... | collective-permute-start | bytes 786440 | tf_op jit(solution)/shard_map/ppermute | solution.py:385
  11.0 4.7 %collective-permute-start.2 = (bf16[2,256,128]{2,1,0:T(8,128)(2,1)S(1)}, bf16[2,256,128]{2,1,0:T(8,128)(2,1)S(1)}, u32[]{:S(2)}, u32[]{:S(2)}) collective-permute-start(bf16[2,256,128]{2,1,0:T(8,128)(2,1)S(1)} %get-tuple-element.27), channel_id=1, source_target_pairs={{1,4},{3,6},{4,1},{5,8},{6,3},{7,10},{8,5},{9,12},{10,7},{11,14},{... | collective-permute-start | bytes 393224 | tf_op jit(solution)/shard_map/ppermute | solution.py:397
  11.7 4.0 %collective-permute-start.1 = (bf16[8,16,128]{2,1,0:T(8,128)(2,1)S(1)}, bf16[8,16,128]{2,1,0:T(8,128)(2,1)S(1)}, u32[]{:S(2)}, u32[]{:S(2)}) collective-permute-start(bf16[8,16,128]{2,1,0:T(8,128)(2,1)S(1)} %get-tuple-element.26), channel_id=1, source_target_pairs={{0,2},{2,0},{1,3},{3,1},{4,6},{6,4},{5,7},{7,5},{8,10},{10,8},{9,1... | collective-permute-start | bytes 98312 | tf_op jit(solution)/shard_map/ppermute | solution.py:402
  13.2 0.7 %collective-permute-start.3 = (bf16[2,16,128]{2,1,0:T(8,128)(2,1)S(1)}, bf16[2,16,128]{2,1,0:T(8,128)(2,1)S(1)}, u32[]{:S(2)}, u32[]{:S(2)}) collective-permute-start(bf16[2,16,128]{2,1,0:T(8,128)(2,1)S(1)} %get-tuple-element.28), channel_id=1, source_target_pairs={{1,6},{3,4},{4,3},{5,10},{6,1},{7,8},{8,7},{9,14},{10,5},{11,12},{... | collective-permute-start | bytes 24584 | tf_op jit(solution)/shard_map/ppermute | solution.py:397
  18.3 5.4 %collective-permute-start.6 = (bf16[4,272,128]{2,1,0:T(8,128)(2,1)S(1)}, bf16[4,272,128]{2,1,0:T(8,128)(2,1)S(1)}, u32[]{:S(2)}, u32[]{:S(2)}) collective-permute-start(bf16[4,272,128]{2,1,0:T(8,128)(2,1)S(1)} %all-to-all-done.block_ref), channel_id=1, source_target_pairs={{0,1},{1,0},{2,3},{3,2},{4,5},{5,4},{6,7},{7,6},{8,9},{9,8},{10,11... | collective-permute-start | bytes 835592 | tf_op jit(solution)/shard_map/ppermute | solution.py:385
  22.3 1.4 %collective-permute-start.4 = (bf16[2,256,128]{2,1,0:T(8,128)(2,1)S(1)}, bf16[2,256,128]{2,1,0:T(8,128)(2,1)S(1)}, u32[]{:S(2)}, u32[]{:S(2)}) collective-permute-start(bf16[2,256,128]{2,1,0:T(8,128)(2,1)S(1)} %collective-permute-done.2.mine_ref), channel_id=1, source_target_pairs={{0,1},{1,0},{2,3},{3,2},{4,5},{5,4},{6,7},{7,6},{8,9},{9,8},{10,11... | collective-permute-start | bytes 393224 | tf_op jit(solution)/shard_map/ppermute | solution.py:385
  22.4 1.3 %collective-permute-start.5 = (bf16[2,16,128]{2,1,0:T(8,128)(2,1)S(1)}, bf16[2,16,128]{2,1,0:T(8,128)(2,1)S(1)}, u32[]{:S(2)}, u32[]{:S(2)}) collective-permute-start(bf16[2,16,128]{2,1,0:T(8,128)(2,1)S(1)} %collective-permute-done.3.mine_tail_ref), channel_id=1, source_target_pairs={{0,1},{1,0},{2,3},{3,2},{4,5},{5,4},{6,7},{7,6},{8,9},{9,8},{10,11... | collective-permute-start | bytes 24584 | tf_op jit(solution)/shard_map/ppermute | solution.py:385
  23.7 18.4 %copy-start.3 = (s32[4]{0:T(128)S(1)}, s32[4]{0:T(128)}, u32[]{:S(2)}) copy-start(s32[4]{0:T(128)} %dest_ref.1) | copy-start | bytes 52
  27.5 0.7 %copy-start.2 = (bf16[8,64,128]{2,1,0:T(8,128)(2,1)}, bf16[8,64,128]{2,1,0:T(8,128)(2,1)S(1)}, u32[]{:S(2)}) copy-start(bf16[8,64,128]{2,1,0:T(8,128)(2,1)S(1)} %get-tuple-element.45) | copy-start | bytes 393220
  28.1 10.9 %collective-permute-start.8 = (bf16[2,256,128]{2,1,0:T(8,128)(2,1)S(1)}, bf16[2,256,128]{2,1,0:T(8,128)(2,1)S(1)}, u32[]{:S(2)}, u32[]{:S(2)}) collective-permute-start(bf16[2,256,128]{2,1,0:T(8,128)(2,1)S(1)} %get-tuple-element.38), channel_id=1, source_target_pairs={{1,4},{3,6},{4,1},{5,8},{6,3},{7,10},{8,5},{9,12},{10,7},{11,14},{... | collective-permute-start | bytes 393224 | tf_op jit(solution)/shard_map/ppermute | solution.py:397
  28.8 13.2 %all-to-all-start.1 = ((bf16[8,64,128]{2,1,0:T(8,128)(2,1)}), bf16[8,64,128]{2,1,0:T(8,128)(2,1)S(1)}, u32[]{:S(2)}, u32[]{:S(2)}) async-start(bf16[8,64,128]{2,1,0:T(8,128)(2,1)} %copy-done.2), calls=%async_computation.1 | async-start | bytes 262144 | tf_op jit(solution)/shard_map/all_to_all | solution.py:502
  35.1 3.9 %collective-permute-start.7 = (bf16[8,16,128]{2,1,0:T(8,128)(2,1)S(1)}, bf16[8,16,128]{2,1,0:T(8,128)(2,1)S(1)}, u32[]{:S(2)}, u32[]{:S(2)}) collective-permute-start(bf16[8,16,128]{2,1,0:T(8,128)(2,1)S(1)} %get-tuple-element.37), channel_id=1, source_target_pairs={{0,2},{2,0},{1,3},{3,1},{4,6},{6,4},{5,7},{7,5},{8,10},{10,8},{9,1... | collective-permute-start | bytes 98312 | tf_op jit(solution)/shard_map/ppermute | solution.py:402
  35.7 0.7 %collective-permute-start.9 = (bf16[2,16,128]{2,1,0:T(8,128)(2,1)S(1)}, bf16[2,16,128]{2,1,0:T(8,128)(2,1)S(1)}, u32[]{:S(2)}, u32[]{:S(2)}) collective-permute-start(bf16[2,16,128]{2,1,0:T(8,128)(2,1)S(1)} %get-tuple-element.39), channel_id=1, source_target_pairs={{1,6},{3,4},{4,3},{5,10},{6,1},{7,8},{8,7},{9,14},{10,5},{11,12},{... | collective-permute-start | bytes 24584 | tf_op jit(solution)/shard_map/ppermute | solution.py:397
  39.0 4.2 %collective-permute-start.10 = (bf16[2,256,128]{2,1,0:T(8,128)(2,1)S(1)}, bf16[2,256,128]{2,1,0:T(8,128)(2,1)}, u32[]{:S(2)}, u32[]{:S(2)}) collective-permute-start(bf16[2,256,128]{2,1,0:T(8,128)(2,1)S(1)} %collective-permute-done.8.mine_ref), channel_id=1, source_target_pairs={{0,1},{1,0},{2,3},{3,2},{4,5},{5,4},{6,7},{7,6},{8,9},{9,8},{10,11... | collective-permute-start | bytes 393224 | tf_op jit(solution)/shard_map/ppermute | solution.py:385
  42.0 1.3 %collective-permute-start.11 = (bf16[2,16,128]{2,1,0:T(8,128)(2,1)S(1)}, bf16[2,16,128]{2,1,0:T(8,128)(2,1)S(1)}, u32[]{:S(2)}, u32[]{:S(2)}) collective-permute-start(bf16[2,16,128]{2,1,0:T(8,128)(2,1)S(1)} %collective-permute-done.9.mine_tail_ref), channel_id=1, source_target_pairs={{0,1},{1,0},{2,3},{3,2},{4,5},{5,4},{6,7},{7,6},{8,9},{9,8},{10,11... | collective-permute-start | bytes 24584 | tf_op jit(solution)/shard_map/ppermute | solution.py:385
